TPU v7x, 32 devices: a whole 2x2x4 slice. The times are simulated.
32 devices in a mesh: row: 4 (over x, core), col: 8 (over z, y).
Axes of the slice: x: 2, y: 2, z: 4, core: 2. Of those that a mesh axis runs over, the one named last changes fastest.
Arguments:
- ancestor_order: int32 [2, 48], replicated, may hold values from 0 to 47, each once within a row
- factor_rows: bfloat16 [2, 24576, 512], P(None, ('row', 'col')), may hold values from -0.0390625 to 0.0390625
- factor_inverse: bfloat16 [2, 512, 512], replicated
- ancestor_inverse: bfloat16 [24576, 24576], P('col', 'row'), may hold values from -6 to 6
- diagonal_inverse: float32 [2, 512, 512], P(None, None, 'row'), may hold values from -6 to 6
Outputs:
- offdiag_inverse: bfloat16 [2, 24576, 512], P(None, 'col', 'row')
- diag_updated: float32 [2, 512, 512], P(None, None, 'row')
Inputs may be any that keep to these rules, and one draw needn't show every extreme that they name: `ancestor_order`: each row lists every ancestor block once; its first 40 entries are the blocks coupled to that supernode.
All inputs are finite; a program needn't handle non-finite values.
Results may differ from a plain program's by a relative error of at most 0.011.
Values may be sent and summed in bfloat16 or wider, within the bound.
A program may use at most 128 MiB of HBM per device.

v0:
```python
import functools

import jax
import jax.numpy as jnp
from jax import lax
from jax.experimental import pallas as pl
from jax.experimental.pallas import tpu as pltpu
from jax.sharding import PartitionSpec as P

NSEL = 40
MESH = pl.DeviceIdType.MESH


def kernel(
    dims, strips, order_ref, factor_ref, inverse_ref, diag_ref, a_ref, out_ref, updated_ref,
    panel, abuf, acc, s1, r1, s2, r2, kept, below, cs, cr, total, sums, turned,
    a_sem, ring_s, ring_r, s1s, r1s, s2s, r2s, bel_s, bel_r, bel_l, cs_s, cs_r, ag_s, ag_r,
):
    chips, n, depth = dims
    supers, piece, block = factor_ref.shape
    chunks = supers * 2
    rows, wide = acc.shape[1], acc.shape[2]
    width = wide // chips
    half = piece // 2
    tall = rows // 4
    per_slab = rows // piece
    slabs = n // per_slab
    r = lax.axis_index("row")
    c = lax.axis_index("col")
    x, k = r // 2, r % 2
    mate = x * 2 + 1 - k
    source_row = c // slabs
    source_x, source_k = source_row // 2, source_row % 2
    length = n // depth

    def col_at(pos):
        y, i = pos // length, pos % length
        return (i + (y % 2) * (length - 1 - 2 * i)) * depth + y

    y, z = c % depth, c // depth
    pos = y * length + z + (y % 2) * (length - 1 - 2 * z)
    right, left = col_at((pos + 1) % n), col_at((pos + n - 1) % n)

    def a_copy(i):
        src = place(i)[4]
        if strips:
            view = a_ref.at[src]
        else:
            view = a_ref.at[:, pl.ds(pl.multiple_of(src * piece, piece), piece)]
        return pltpu.make_async_copy(view, abuf.at[i % 2], a_sem.at[i % 2])

    def place(i):
        g, j = i // n, i % n
        t = (j + 1) // 2
        last = j // (n - 1)
        d = last * (g % 2) + (1 - last) * (1 - j % 2)
        return g, j, t, d, col_at((pos + (2 * d - 1) * t + n) % n)

    def ring(g, t, d, h, src):
        view = panel.at[g, src, pl.ds(h * half, half)]
        return pltpu.make_async_remote_copy(
            src_ref=view, dst_ref=view,
            send_sem=ring_s.at[d, g, t - 1, h], recv_sem=ring_r.at[d, g, t - 1, h],
            device_id=(r, right * (1 - d) + left * d), device_id_type=MESH,
        )

    def coupled(s, first, count):
        low = order_ref[pl.ds(s, 1), 0:NSEL] * block
        label = first + lax.broadcasted_iota(jnp.int32, (count, NSEL), 0)
        return jnp.sum(jnp.where((label >= low) & (label < low + block), 1.0, 0.0), axis=1, keepdims=True)

    def norm(g):
        s, p = g // 2, g % 2
        keep = coupled(s, (r * n + c) * piece, piece)
        for b in range(chips):
            at = pl.ds((2 * b + p) * width, width)
            term = jnp.dot(factor_ref[s], inverse_ref[s, :, at], preferred_element_type=jnp.float32)
            panel[g, c, :, pl.ds(b * width, width)] = (term * keep).astype(jnp.bfloat16)

    def below_copy(g, src, i, to_row, sem):
        return pltpu.make_async_remote_copy(
            src_ref=src, dst_ref=below.at[g, i], send_sem=sem, recv_sem=bel_r.at[g, i],
            device_id=(to_row, c), device_id_type=MESH,
        )

    def tile(m):
        return pl.ds(pl.multiple_of(m * tall, tall), tall)

    def first_copy(s, b, m):
        return pltpu.make_async_remote_copy(
            src_ref=s1.at[s, b, tile(m)], dst_ref=r1.at[s, b, tile(m)],
            send_sem=s1s.at[s, b, m], recv_sem=r1s.at[s, b, m],
            device_id=(mate, c), device_id_type=MESH,
        )

    def second_copy(s, b, m, slot):
        return pltpu.make_async_remote_copy(
            src_ref=s2.at[s, b, tile(m)], dst_ref=r2.at[s, slot, tile(m)],
            send_sem=s2s.at[s, b, m], recv_sem=r2s.at[s, slot, m],
            device_id=(b * 2 + k, c), device_id_type=MESH,
        )

    def stage1(g, m):
        s = g // 2
        for b in range(chips):
            s1[s, b, tile(m), :] = acc[g % 2, tile(m), pl.ds(b * width, width)].astype(jnp.bfloat16)
            first_copy(s, b, m).start()

    def stage2(g):
        s = g // 2

        @pl.when(k == g % 2)
        def _():
            @pl.loop(0, 4)
            def _(m):
                for b in range(chips):
                    first_copy(s, b, m).wait_recv()
                    both = acc[g % 2, tile(m), pl.ds(b * width, width)] + r1[s, b, tile(m), :].astype(jnp.float32)

                    @pl.when(x == b)
                    def _():
                        kept[s, tile(m), :] = both

                    @pl.when(x != b)
                    def _():
                        s2[s, b, tile(m), :] = both.astype(jnp.bfloat16)
                        second_copy(s, b, m, x).start()

    def stage3(g):
        s = g // 2

        @pl.when(k == g % 2)
        def _():
            @pl.loop(0, 4)
            def _(m):
                for b in range(chips):
                    @pl.when(x != b)
                    def _():
                        second_copy(s, b, m, b).wait_recv()
                        kept[s, tile(m), :] += r2[s, b, tile(m), :].astype(jnp.float32)
                keep = coupled(s, c * rows + m * tall, tall)
                out_ref[s, tile(m), :] = (-(kept[s, tile(m), :] * keep)).astype(jnp.bfloat16)

    def pass_below(g):
        @pl.when((k == source_k) & (x != source_x))
        def _():
            for i in range(per_slab):
                below_copy(g, below.at[g, i], i, mate, bel_s.at[g, i, chips]).wait_recv()
                below_copy(g, below.at[g, i], i, mate, bel_s.at[g, i, chips]).start()

    def scatter(s, delta):
        to = (c + delta) % n
        return pltpu.make_async_remote_copy(
            src_ref=cs.at[s, to], dst_ref=cr.at[s, delta],
            send_sem=cs_s.at[s, delta], recv_sem=cs_r.at[s, delta],
            device_id=(r, to), device_id_type=MESH,
        )

    def gather(s, delta, slot):
        return pltpu.make_async_remote_copy(
            src_ref=total.at[s], dst_ref=sums.at[s, slot],
            send_sem=ag_s.at[s, delta], recv_sem=ag_r.at[s, delta],
            device_id=(r, (c + delta) % n), device_id_type=MESH,
        )

    def wait_below(s):
        for q in range(2):
            for i in range(per_slab):
                g = 2 * s + q

                @pl.when(r == source_row)
                def _():
                    pltpu.make_async_copy(panel.at[g, c], below.at[g, i], bel_l.at[g, i]).wait()

                @pl.when(k != source_k)
                def _():
                    below_copy(g, below.at[g, i], i, mate, bel_s.at[g, i, chips]).wait_recv()

    def correct(s):
        for q in range(2):
            term = jnp.zeros((width, wide), jnp.float32)
            for i in range(per_slab):
                term -= lax.dot_general(
                    out_ref[s, pl.ds(i * piece, piece), :], below[2 * s + q, i],
                    (((0,), (0,)), ((), ())), preferred_element_type=jnp.float32,
                )
            for b in range(n):
                cs[s, b, q] = term[b * part:(b + 1) * part, :].astype(jnp.bfloat16)
        for delta in range(1, n):
            scatter(s, delta).start()

    def collect(s):
        summed = cs[s, c].astype(jnp.float32)
        for delta in range(1, n):
            scatter(s, delta).wait_recv()
            summed += cr[s, delta].astype(jnp.float32)
        total[s] = summed.astype(jnp.bfloat16)
        for delta in range(1, n):
            gather(s, delta, c).start()
        sums[s, c] = summed.astype(jnp.bfloat16)

    def update(s):
        for delta in range(1, n):
            gather(s, delta, (c + n - delta) % n).wait_recv()
        for q in range(2):
            for b in range(n):
                turned[b * part:(b + 1) * part, :] = sums[s, b, q].astype(jnp.float32)
            term = turned[...].T
            for b in range(chips):
                at = pl.ds((2 * b + q) * width, width)
                updated_ref[s, at, :] = diag_ref[s, at, :] + term[b * width:(b + 1) * width, :]

    part = width // n
    barrier = pltpu.get_barrier_semaphore()
    for delta in range(1, n):
        pl.semaphore_signal(barrier, inc=1, device_id=(r, (c + delta) % n), device_id_type=MESH)
    pl.semaphore_signal(barrier, inc=1, device_id=(mate, c), device_id_type=MESH)
    for delta in range(1, chips):
        pl.semaphore_signal(barrier, inc=1, device_id=(((x + delta) % chips) * 2 + k, c), device_id_type=MESH)
    a_copy(0).start()
    norm(0)
    pl.semaphore_wait(barrier, n - 1 + 1 + chips - 1)
    for h in range(2):
        for d in range(2):
            ring(0, 1, d, h, c).start()
    for g in range(1, chunks):
        norm(g)

    @pl.loop(0, chunks * n)
    def _(i):
        g, j, t, d, src = place(i)

        ahead, h = j // 2 + 1, j % 2
        for way in range(2):
            @pl.when((ahead < n // 2) | (way == g % 2))
            def _():
                come = col_at((pos + (2 * way - 1) * ahead + n) % n)
                ring(g, ahead, way, h, come).wait_recv()

                @pl.when((ahead + 1 < n // 2) | ((ahead + 1 == n // 2) & (way == g % 2)))
                def _():
                    ring(g, ahead + 1, way, h, come).start()

            @pl.when((g < chunks - 1) & (j == n - 5 + 2 * ((g + way + 1) % 2)))
            def _():
                for first in range(2):
                    ring(g + 1, 1, way, first, c).start()

        @pl.when((r == source_row) & (src // per_slab == c % slabs))
        def _():
            at = src % per_slab
            for delta in range(1, chips):
                to = ((x + delta) % chips) * 2 + k
                below_copy(g, panel.at[g, src], at, to, bel_s.at[g, at, delta]).start()
            below_copy(g, panel.at[g, src], at, mate, bel_s.at[g, at, chips]).start()
            pltpu.make_async_copy(panel.at[g, src], below.at[g, at], bel_l.at[g, at]).start()

        a_copy(i).wait()

        @pl.when(i + 1 < chunks * n)
        def _():
            a_copy(i + 1).start()

        slot = i % 2

        @pl.loop(0, 4)
        def _(m):
            at = pl.ds(pl.multiple_of(m * tall, tall), tall)
            term = jnp.dot(abuf[slot, at, :], panel[g, src], preferred_element_type=jnp.float32)

            @pl.when(j == 0)
            def _():
                acc[g % 2, at, :] = term

            @pl.when(j > 0)
            def _():
                acc[g % 2, at, :] += term

            @pl.when((j == n - 1) & (k != g % 2))
            def _():
                stage1(g, m)

        @pl.when((j == 1) & (g > 0))
        def _():
            stage2(g - 1)

        @pl.when((j == 3) & (g > 0))
        def _():
            pass_below(g - 1)

        @pl.when((j == n - 3) & (g > 0))
        def _():
            stage3(g - 1)

        @pl.when((j == 2) & (g >= 3) & (g % 2 == 1))
        def _():
            wait_below((g - 3) // 2)
            correct((g - 3) // 2)

        @pl.when((j == n - 2) & (g >= 3) & (g % 2 == 1))
        def _():
            collect((g - 3) // 2)

    stage2(chunks - 1)
    pass_below(chunks - 1)
    wait_below(supers - 1)
    stage3(chunks - 1)
    correct(supers - 1)
    for s in range(supers - 1):
        update(s)
    collect(supers - 1)
    update(supers - 1)
    for s in range(supers):
        for delta in range(1, n):
            scatter(s, delta).wait_send()
            gather(s, delta, c).wait_send()

    @pl.loop(0, chunks)
    def _(g):
        @pl.loop(1, n // 2 + 1)
        def _(t):
            for d in range(2):
                @pl.when((t < n // 2) | (d == g % 2))
                def _():
                    for h in range(2):
                        ring(g, t, d, h, c).wait_send()

        for i in range(per_slab):
            @pl.when(r == source_row)
            def _():
                for delta in range(1, chips):
                    below_copy(g, panel.at[g, c], i, mate, bel_s.at[g, i, delta]).wait_send()
                below_copy(g, panel.at[g, c], i, mate, bel_s.at[g, i, chips]).wait_send()

            @pl.when((k == source_k) & (x != source_x))
            def _():
                below_copy(g, below.at[g, i], i, mate, bel_s.at[g, i, chips]).wait_send()

    for s in range(supers):
        for b in range(chips):
            @pl.loop(0, 4)
            def _(m):
                first_copy(s, b, m).wait_send()

                @pl.when(x != b)
                def _():
                    second_copy(s, b, m, x).wait_send()


def body(ancestor_order, factor_rows, factor_inverse, ancestor_inverse, diagonal_inverse):
    supers, piece, block = factor_rows.shape
    rows = ancestor_inverse.shape[0]
    row_count, n = lax.axis_size("row"), lax.axis_size("col")
    chips = row_count // 2
    depth = chips
    width = block // row_count
    wide = chips * width
    chunks = supers * 2

    strips = piece % 128 != 0
    left = ancestor_inverse
    if strips:
        left = left.reshape(rows, n, piece).transpose(1, 0, 2)
    per_slab = rows // piece
    part = width // n
    half_type, full_type, dma = jnp.bfloat16, jnp.float32, pltpu.SemaphoreType.DMA
    return pl.pallas_call(
        functools.partial(kernel, (chips, n, depth), strips),
        out_shape=(
            jax.ShapeDtypeStruct((supers, rows, width), half_type),
            jax.ShapeDtypeStruct((supers, block, width), full_type),
        ),
        in_specs=[pl.BlockSpec(memory_space=pltpu.VMEM)] * 4 + [pl.BlockSpec(memory_space=pl.ANY)],
        out_specs=(pl.BlockSpec(memory_space=pltpu.VMEM),) * 2,
        scratch_shapes=[
            pltpu.VMEM((chunks, n, piece, wide), half_type),
            pltpu.VMEM((2, rows, piece), half_type),
            pltpu.VMEM((2, rows, wide), full_type),
            pltpu.VMEM((supers, chips, rows, width), half_type),
            pltpu.VMEM((supers, chips, rows, width), half_type),
            pltpu.VMEM((supers, chips, rows, width), half_type),
            pltpu.VMEM((supers, chips, rows, width), half_type),
            pltpu.VMEM((supers, rows, width), full_type),
            pltpu.VMEM((chunks, per_slab, piece, wide), half_type),
            pltpu.VMEM((supers, n, 2, part, wide), half_type),
            pltpu.VMEM((supers, n, 2, part, wide), half_type),
            pltpu.VMEM((supers, 2, part, wide), half_type),
            pltpu.VMEM((supers, n, 2, part, wide), half_type),
            pltpu.VMEM((width, wide), full_type),
            dma((2,)),
            dma((2, chunks, n // 2, 2)),
            dma((2, chunks, n // 2, 2)),
            dma((supers, chips, 4)),
            dma((supers, chips, 4)),
            dma((supers, chips, 4)),
            dma((supers, chips, 4)),
            dma((chunks, per_slab, chips + 1)),
            dma((chunks, per_slab)),
            dma((chunks, per_slab)),
            dma((supers, n)),
            dma((supers, n)),
            dma((supers, n)),
            dma((supers, n)),
        ],
        compiler_params=pltpu.CompilerParams(
            collective_id=0, has_side_effects=True, vmem_limit_bytes=64 * 1024 * 1024 - 65536
        ),
        cost_estimate=pl.CostEstimate(
            flops=2 * rows * n * piece * supers * block, bytes_accessed=8 * rows * n * piece, transcendentals=0
        ),
    )(ancestor_order, factor_rows, factor_inverse, diagonal_inverse, left)


def solution(mesh):
    placed = (P(), P(None, ("row", "col"), None), P(), P("col", "row"), P(None, None, "row"))
    return jax.shard_map(
        body,
        mesh=mesh,
        in_specs=placed,
        out_specs=(P(None, "col", "row"), P(None, None, "row")),
        check_vma=False,
    )
```

profile of v0, /device:TPU:1, one launch (start us, length us, event | category | flops | bytes accessed | tf_op | source)
XLA Modules:
  0.0 170.3 jit_solution(8692638809188137046)
XLA Ops:
  0.6 166.1 %shard_map.68 = (bf16[2,3072,128]{2,1,0:T(8,128)(2,1)}, f32[2,512,128]{2,1,0:T(8,128)}) custom-call(s32[2,48]{1,0:T(2,128)} %order_ref.1, bf16[2,768,512]{2,1,0:T(8,128)(2,1)} %factor_ref.1, bf16[2,512,512]{2,1,0:T(8,128)(2,1)} %inverse_ref.1, f32[2,512,128]{2,1,0:T(8,128)} %diag_ref.1, bf16[3072,6144]{1,0:T(8,128)(2,1)} %a_ref.1), custom_call_target="tpu_custom_call" | custom-call | flops 38654705664 | bytes 150994944 | tf_op jit(solution)/shard_map/pallas_call | solution.py:367
  166.7 0.0 copy-start
  166.7 2.7 %copy.9 = bf16[2,3072,128]{2,1,0:T(8,128)(2,1)} copy(bf16[2,3072,128]{2,1,0:T(8,128)(2,1)} %get-tuple-element.4) | data formatting | bytes 3145728
  169.5 0.0 copy-done
  169.5 0.8 copy.10
Async XLA Ops:
  166.7 2.7 %copy-start = (f32[2,512,128]{2,1,0:T(8,128)S(1)}, f32[2,512,128]{2,1,0:T(8,128)}, u32[]{:S(2)}) copy-start(f32[2,512,128]{2,1,0:T(8,128)} %get-tuple-element.5) | copy-start | bytes 1572868
where the time goes:
time: 170 us
  Pallas kernels  166 us (98%)
  local copies, waits for them, and re-layouts  3.51 us (2%)
    pallas_call x1, Pallas kernels, body(): pl.pallas_call(functools.partial(kernel, (chips, n, depth), strips), out_...  166 us
    unnamed x4, local copies, waits for them, and re-layouts  3.51 us

commit v1 on v0

v1 whole, which is shorter than its diff:
```python
import functools

import jax
import jax.numpy as jnp
from jax import lax
from jax.experimental import pallas as pl
from jax.experimental.pallas import tpu as pltpu
from jax.sharding import PartitionSpec as P

NSEL = 40
MESH = pl.DeviceIdType.MESH
TILES = 4
LAG = 4


def kernel(
    dims, strips, order_ref, factor_hbm, inverse_hbm, diag_hbm, a_ref, out_hbm, updated_hbm,
    factor, inverse, diag, outs, updated, panel, abuf, acc, s1, r1, s2, r2, kept, below, cs, cr, total, sums, gsum,
    in_sem, o_sem, a_sem, ring_s, ring_r, s1s, r1s, s2s, r2s, bel_s, bel_r, bel_l, cs_s, cs_r, ag_s, ag_r,
):
    chips, n, depth = dims
    supers, piece, block = factor.shape
    rows, pair = acc.shape[1], acc.shape[2]
    width = pair // 2
    chunks = supers * chips
    half = piece // 2
    tall = rows // TILES
    per_slab = rows // piece
    slabs = n // per_slab
    part = width // n
    r = lax.axis_index("row")
    c = lax.axis_index("col")
    x, k = r // 2, r % 2
    mate = x * 2 + 1 - k
    source_row = c // slabs
    source_x, source_k = source_row // 2, source_row % 2
    source = r == source_row
    passing = (k == source_k) & (x != source_x)
    length = n // depth
    steps = chunks * n

    def col_at(pos):
        y, i = pos // length, pos % length
        return (i + (y % 2) * (length - 1 - 2 * i)) * depth + y

    y, z = c % depth, c // depth
    pos = y * length + z + (y % 2) * (length - 1 - 2 * z)
    right, left = col_at((pos + 1) % n), col_at((pos + n - 1) % n)

    def src_of(j):
        t = (j + 1) // 2
        return col_at((pos + (1 - 2 * (j % 2)) * t + n) % n)

    def a_copy(i):
        src = src_of(i % n)
        if strips:
            view = a_ref.at[src]
        else:
            view = a_ref.at[:, pl.ds(pl.multiple_of(src * piece, piece), piece)]
        return pltpu.make_async_copy(view, abuf.at[i % 2], a_sem.at[i % 2])

    def block_of(g, at_x):
        return (at_x + 1 + g // supers) % chips

    def slot_of(g):
        return (g % supers) * chips + block_of(g, source_x)

    def ring(g, t, d, h, src):
        view = panel.at[g, src, pl.ds(h * half, half)]
        return pltpu.make_async_remote_copy(
            src_ref=view, dst_ref=view,
            send_sem=ring_s.at[d, g, t - 1, h], recv_sem=ring_r.at[d, g, t - 1, h],
            device_id=(r, right * (1 - d) + left * d), device_id_type=MESH,
        )

    def coupled(s, first, count):
        low = order_ref[pl.ds(s, 1), 0:NSEL] * block
        label = first + lax.broadcasted_iota(jnp.int32, (count, NSEL), 0)
        return jnp.sum(jnp.where((label >= low) & (label < low + block), 1.0, 0.0), axis=1, keepdims=True)

    def norm(g, h):
        s = g % supers
        keep = coupled(s, (r * n + c) * piece + h * half, half)
        at = pl.ds(pl.multiple_of(block_of(g, x) * pair, pair), pair)
        term = jnp.dot(factor[s, h * half:(h + 1) * half, :], inverse[s, :, at], preferred_element_type=jnp.float32)
        panel[g, c, h * half:(h + 1) * half, :] = (term * keep).astype(jnp.bfloat16)

    def below_copy(slot, at, src, to_row, sem):
        return pltpu.make_async_remote_copy(
            src_ref=src, dst_ref=below.at[slot, at], send_sem=sem, recv_sem=bel_r.at[slot, at],
            device_id=(to_row, c), device_id_type=MESH,
        )

    def below_here(slot, at, g, src):
        return pltpu.make_async_copy(panel.at[g, src], below.at[slot, at], bel_l.at[slot, at])

    def pass_below(i):
        g, src = i // n, src_of(i % n)
        slot, at = slot_of(g), src % per_slab

        @pl.when(passing & (src // per_slab == c % slabs))
        def _():
            copy = below_copy(slot, at, below.at[slot, at], mate, bel_s.at[slot, at, chips])
            copy.wait_recv()
            copy.start()

    def tile(m):
        return pl.ds(pl.multiple_of(m * tall, tall), tall)

    def mate_copy(g, m):
        return pltpu.make_async_remote_copy(
            src_ref=s1.at[g, tile(m)], dst_ref=r1.at[g, tile(m)],
            send_sem=s1s.at[g, m], recv_sem=r1s.at[g, m],
            device_id=(mate, c), device_id_type=MESH,
        )

    def cross_copy(g, m, slot):
        s = g % supers
        return pltpu.make_async_remote_copy(
            src_ref=s2.at[g, tile(m)], dst_ref=r2.at[s, slot, tile(m)],
            send_sem=s2s.at[g, m], recv_sem=r2s.at[s, slot, m],
            device_id=(block_of(g, x) * 2 + k, c), device_id_type=MESH,
        )

    def give(g, m):
        theirs = jnp.where(k == 0, acc[g % 2, tile(m), width:], acc[g % 2, tile(m), :width])
        s1[g, tile(m), :] = theirs.astype(jnp.bfloat16)
        mate_copy(g, m).start()

    def both(g, m):
        mate_copy(g, m).wait_recv()
        mine = jnp.where(k == 0, acc[g % 2, tile(m), :width], acc[g % 2, tile(m), width:])
        return mine + r1[g, tile(m), :].astype(jnp.float32)

    def send_across(g):
        @pl.loop(0, TILES)
        def _(m):
            s2[g, tile(m), :] = both(g, m).astype(jnp.bfloat16)
            cross_copy(g, m, x).start()

    def out_copy(s):
        return pltpu.make_async_copy(outs.at[s], out_hbm.at[s], o_sem.at[s])

    def finish(g, s):
        @pl.loop(0, TILES)
        def _(m):
            whole = both(g, m)
            for delta in range(1, chips):
                slot = (x + delta) % chips
                cross_copy(s, m, slot).wait_recv()
                whole += r2[s, slot, tile(m), :].astype(jnp.float32)
            outs[s, tile(m), :] = (-(whole * kept[s, tile(m), :])).astype(jnp.bfloat16)

    def scatter(s, delta):
        to = (c + delta) % n
        return pltpu.make_async_remote_copy(
            src_ref=cs.at[s, to], dst_ref=cr.at[s, delta],
            send_sem=cs_s.at[s, delta], recv_sem=cs_r.at[s, delta],
            device_id=(r, to), device_id_type=MESH,
        )

    def gather(s, delta, slot):
        return pltpu.make_async_remote_copy(
            src_ref=total.at[s], dst_ref=sums.at[s, slot],
            send_sem=ag_s.at[s, delta], recv_sem=ag_r.at[s, delta],
            device_id=(r, (c + delta) % n), device_id_type=MESH,
        )

    def correct(s, first, last):
        @pl.loop(first, last)
        def _(j):
            src = src_of(j)
            at = src % per_slab

            @pl.when(src // per_slab == c % slabs)
            def _():
                for e in range(chips):
                    g = e * supers + s
                    slot = slot_of(g)

                    @pl.when(source)
                    def _():
                        below_here(slot, at, g, src).wait()

                    @pl.when(k != source_k)
                    def _():
                        below_copy(slot, at, below.at[slot, at], mate, bel_s.at[slot, at, chips]).wait_recv()

                left = outs[s, pl.ds(pl.multiple_of(at * piece, piece), piece), :]
                for b in range(chips):
                    gsum[:, b * pair:(b + 1) * pair] -= lax.dot_general(
                        left, below[s * chips + b, at], (((0,), (0,)), ((), ())), preferred_element_type=jnp.float32
                    )

    def spread(s):
        for b in range(n):
            cs[s, b] = gsum[b * part:(b + 1) * part, :].astype(jnp.bfloat16)
        for delta in range(1, n):
            scatter(s, delta).start()

    def collect(s):
        summed = cs[s, c].astype(jnp.float32)
        for delta in range(1, n):
            scatter(s, delta).wait_recv()
            summed += cr[s, delta].astype(jnp.float32)
        total[s] = summed.astype(jnp.bfloat16)
        for delta in range(1, n):
            gather(s, delta, c).start()
        sums[s, c] = summed.astype(jnp.bfloat16)

    def updated_copy(s):
        return pltpu.make_async_copy(updated.at[s], updated_hbm.at[s], o_sem.at[supers + s])

    def update(s):
        for delta in range(1, n):
            gather(s, delta, (c + n - delta) % n).wait_recv()
        for b in range(n):
            gsum[b * part:(b + 1) * part, :] = sums[s, b].astype(jnp.float32)
        updated[s] = diag[s] + gsum[...].T
        updated_copy(s).start()

    def factor_copy(s):
        return pltpu.make_async_copy(factor_hbm.at[s], factor.at[s], in_sem.at[s])

    def inverse_copy(s):
        return pltpu.make_async_copy(inverse_hbm.at[s], inverse.at[s], in_sem.at[supers + s])

    diag_copy = pltpu.make_async_copy(diag_hbm, diag, in_sem.at[2 * supers])

    barrier = pltpu.get_barrier_semaphore()
    for delta in range(1, n):
        pl.semaphore_signal(barrier, inc=1, device_id=(r, (c + delta) % n), device_id_type=MESH)
    pl.semaphore_signal(barrier, inc=1, device_id=(mate, c), device_id_type=MESH)
    for delta in range(1, chips):
        pl.semaphore_signal(barrier, inc=1, device_id=(((x + delta) % chips) * 2 + k, c), device_id_type=MESH)
    for s in range(supers):
        factor_copy(s).start()
        inverse_copy(s).start()
    a_copy(0).start()
    diag_copy.start()
    factor_copy(0).wait()
    inverse_copy(0).wait()
    norm(0, 0)
    pl.semaphore_wait(barrier, n - 1 + 1 + chips - 1)
    for h in range(2):
        if h:
            norm(0, h)
        for d in range(2):
            ring(0, 1, d, h, c).start()
    for s in range(1, supers):
        factor_copy(s).wait()
        inverse_copy(s).wait()
    for g in range(1, chunks):
        for h in range(2):
            norm(g, h)
    for s in range(supers):
        @pl.loop(0, TILES)
        def _(m):
            kept[s, tile(m), :] = jnp.broadcast_to(coupled(s, c * rows + m * tall, tall), (tall, width))

    @pl.loop(0, steps)
    def _(i):
        g, j = i // n, i % n
        src = src_of(j)
        ahead, h = j // 2 + 1, j % 2

        @pl.when(ahead < n // 2)
        def _():
            for way in range(2):
                come = col_at((pos + (2 * way - 1) * ahead + n) % n)
                ring(g, ahead, way, h, come).wait_recv()

                @pl.when((ahead + 1 < n // 2) | (h == way))
                def _():
                    ring(g, ahead + 1, way, h, come).start()

        @pl.when((j == n - 3) & (g < chunks - 1))
        def _():
            for first in range(2):
                for way in range(2):
                    ring(g + 1, 1, way, first, c).start()

        @pl.when(j == n - 1)
        def _():
            for way in range(2):
                ring(g, n // 2, way, way, src).wait_recv()

        @pl.when(source & (src // per_slab == c % slabs))
        def _():
            slot, at = slot_of(g), src % per_slab
            for delta in range(1, chips):
                to = ((x + delta) % chips) * 2 + k
                below_copy(slot, at, panel.at[g, src], to, bel_s.at[slot, at, delta]).start()
            below_copy(slot, at, panel.at[g, src], mate, bel_s.at[slot, at, chips]).start()
            below_here(slot, at, g, src).start()

        @pl.when(i >= LAG)
        def _():
            pass_below(i - LAG)

        a_copy(i).wait()

        @pl.when(i + 1 < steps)
        def _():
            a_copy(i + 1).start()

        @pl.loop(0, TILES)
        def _(m):
            term = jnp.dot(abuf[i % 2, tile(m), :], panel[g, src], preferred_element_type=jnp.float32)

            @pl.when(j == 0)
            def _():
                acc[g % 2, tile(m), :] = term

            @pl.when(j > 0)
            def _():
                acc[g % 2, tile(m), :] += term

            @pl.when(j == n - 1)
            def _():
                give(g, m)

        @pl.when((j == 1) & (g > 0) & (g <= chunks - supers))
        def _():
            send_across(g - 1)

        for s in range(supers - 1):
            own = chunks - supers + s

            @pl.when((j == 1) & (g == own + 1))
            def _():
                finish(own, s)
                out_copy(s).start()

            @pl.when((j == n // 2) & (g == own + 1))
            def _():
                gsum[...] = jnp.zeros_like(gsum)
                correct(s, 0, n)
                spread(s)

            @pl.when((j == n - 2) & (g == own + 1))
            def _():
                collect(s)

    last = supers - 1
    for i in range(steps - LAG, steps - 1):
        pass_below(i)
    finish(chunks - 1, last)
    out_copy(last).start()
    for s in range(supers - 1):
        if s == 0:
            diag_copy.wait()
        update(s)
    gsum[...] = jnp.zeros_like(gsum)
    correct(last, 0, n - 1)
    pass_below(steps - 1)
    correct(last, n - 1, n)
    spread(last)
    if supers == 1:
        diag_copy.wait()
    collect(last)
    update(last)
    for s in range(supers):
        for delta in range(1, n):
            scatter(s, delta).wait_send()
            gather(s, delta, c).wait_send()

    @pl.loop(0, chunks)
    def _(g):
        @pl.loop(1, n // 2 + 1)
        def _(t):
            for d in range(2):
                for h in range(2):
                    @pl.when((t < n // 2) | (h == d))
                    def _():
                        ring(g, t, d, h, c).wait_send()

        slot = slot_of(g)
        for at in range(per_slab):
            @pl.when(source)
            def _():
                for delta in range(1, chips):
                    below_copy(slot, at, panel.at[g, c], mate, bel_s.at[slot, at, delta]).wait_send()
                below_copy(slot, at, panel.at[g, c], mate, bel_s.at[slot, at, chips]).wait_send()

            @pl.when(passing)
            def _():
                below_copy(slot, at, below.at[slot, at], mate, bel_s.at[slot, at, chips]).wait_send()

        for m in range(TILES):
            mate_copy(g, m).wait_send()

            @pl.when(g < chunks - supers)
            def _():
                cross_copy(g, m, x).wait_send()

    for s in range(supers):
        out_copy(s).wait()
        updated_copy(s).wait()


def body(ancestor_order, factor_rows, factor_inverse, ancestor_inverse, diagonal_inverse):
    supers, piece, block = factor_rows.shape
    rows = ancestor_inverse.shape[0]
    row_count, n = lax.axis_size("row"), lax.axis_size("col")
    chips = row_count // 2
    depth = chips
    width = block // row_count
    pair = 2 * width
    chunks = supers * chips

    strips = piece % 128 != 0
    left = ancestor_inverse
    if strips:
        left = left.reshape(rows, n, piece).transpose(1, 0, 2)
    per_slab = rows // piece
    part = width // n
    half_type, full_type, dma = jnp.bfloat16, jnp.float32, pltpu.SemaphoreType.DMA
    anywhere = pl.BlockSpec(memory_space=pl.ANY)
    return pl.pallas_call(
        functools.partial(kernel, (chips, n, depth), strips),
        out_shape=(
            jax.ShapeDtypeStruct((supers, rows, width), half_type),
            jax.ShapeDtypeStruct((supers, block, width), full_type),
        ),
        in_specs=[pl.BlockSpec(memory_space=pltpu.VMEM)] + [anywhere] * 4,
        out_specs=(anywhere,) * 2,
        scratch_shapes=[
            pltpu.VMEM((supers, piece, block), half_type),
            pltpu.VMEM((supers, block, block), half_type),
            pltpu.VMEM((supers, block, width), full_type),
            pltpu.VMEM((supers, rows, width), half_type),
            pltpu.VMEM((supers, block, width), full_type),
            pltpu.VMEM((chunks, n, piece, pair), half_type),
            pltpu.VMEM((2, rows, piece), half_type),
            pltpu.VMEM((2, rows, pair), full_type),
            pltpu.VMEM((chunks, rows, width), half_type),
            pltpu.VMEM((chunks, rows, width), half_type),
            pltpu.VMEM((chunks - supers, rows, width), half_type),
            pltpu.VMEM((supers, chips, rows, width), half_type),
            pltpu.VMEM((supers, rows, width), full_type),
            pltpu.VMEM((chunks, per_slab, piece, pair), half_type),
            pltpu.VMEM((supers, n, part, block), half_type),
            pltpu.VMEM((supers, n, part, block), half_type),
            pltpu.VMEM((supers, part, block), half_type),
            pltpu.VMEM((supers, n, part, block), half_type),
            pltpu.VMEM((width, block), full_type),
            dma((2 * supers + 1,)),
            dma((2 * supers,)),
            dma((2,)),
            dma((2, chunks, n // 2, 2)),
            dma((2, chunks, n // 2, 2)),
            dma((chunks, TILES)),
            dma((chunks, TILES)),
            dma((chunks - supers, TILES)),
            dma((supers, chips, TILES)),
            dma((chunks, per_slab, chips + 1)),
            dma((chunks, per_slab)),
            dma((chunks, per_slab)),
            dma((supers, n)),
            dma((supers, n)),
            dma((supers, n)),
            dma((supers, n)),
        ],
        compiler_params=pltpu.CompilerParams(
            collective_id=0, has_side_effects=True, vmem_limit_bytes=64 * 1024 * 1024 - 65536
        ),
        cost_estimate=pl.CostEstimate(
            flops=2 * rows * n * piece * supers * block, bytes_accessed=8 * rows * n * piece, transcendentals=0
        ),
    )(ancestor_order, factor_rows, factor_inverse, diagonal_inverse, left)


def solution(mesh):
    placed = (P(), P(None, ("row", "col"), None), P(), P("col", "row"), P(None, None, "row"))
    return jax.shard_map(
        body,
        mesh=mesh,
        in_specs=placed,
        out_specs=(P(None, "col", "row"), P(None, None, "row")),
        check_vma=False,
    )
```

time: 170 us -> 164 us (0.965)
  Pallas kernels: 166 us -> 159 us
    pallas_call x1, Pallas kernels: 166 us -> 159 us  [body(): pl.pallas_call(functools.partial(kernel, (chips, n, depth), strips), out_...]
where the time goes in v1:
time: 164 us; the launch traced here: 163 us
  Pallas kernels  159 us (97%)
  local copies, waits for them, and re-layouts  3.51 us (2%)
    pallas_call x1, Pallas kernels, body(): pl.pallas_call(functools.partial(kernel, (chips, n, depth), strips), out_...  159 us
    unnamed x4, local copies, waits for them, and re-layouts  3.51 us

profile of v1, /device:TPU:1, one launch (start us, length us, event | category | flops | bytes accessed | tf_op | source)
XLA Modules:
  0.0 163.1 jit_solution(2744147853904109228)
XLA Ops:
  0.6 159.0 %shard_map.68 = (bf16[2,3072,128]{2,1,0:T(8,128)(2,1)}, f32[2,512,128]{2,1,0:T(8,128)}) custom-call(s32[2,48]{1,0:T(2,128)} %order_ref.1, bf16[2,768,512]{2,1,0:T(8,128)(2,1)} %factor_hbm.1, bf16[2,512,512]{2,1,0:T(8,128)(2,1)} %inverse_hbm.1, f32[2,512,128]{2,1,0:T(8,128)} %diag_hbm.1, bf16[3072,6144]{1,0:T(8,128)(2,1)} %a_ref.1), custom_call_target="tpu_custom_call" | custom-call | flops 38654705664 | bytes 150994944 | tf_op jit(solution)/shard_map/pallas_call | solution.py:420
  159.6 0.0 copy-start
  159.6 2.7 %copy.9 = bf16[2,3072,128]{2,1,0:T(8,128)(2,1)} copy(bf16[2,3072,128]{2,1,0:T(8,128)(2,1)} %get-tuple-element.4) | data formatting | bytes 3145728
  162.3 0.0 copy-done
  162.3 0.8 copy.10
Async XLA Ops:
  159.6 2.7 %copy-start = (f32[2,512,128]{2,1,0:T(8,128)S(1)}, f32[2,512,128]{2,1,0:T(8,128)}, u32[]{:S(2)}) copy-start(f32[2,512,128]{2,1,0:T(8,128)} %get-tuple-element.5) | copy-start | bytes 1572868

commit v2 on v1

v2 whole, which is shorter than its diff:
```python
import functools

import jax
import jax.numpy as jnp
from jax import lax
from jax.experimental import pallas as pl
from jax.experimental.pallas import tpu as pltpu
from jax.sharding import PartitionSpec as P

NSEL = 40
MESH = pl.DeviceIdType.MESH
TILES = 2
LAG = 6
NEAR = 2
BEGIN = 2
DEEP = 3


def kernel(
    dims, strips, order_ref, factor_hbm, inverse_hbm, diag_hbm, a_ref, out_hbm, updated_hbm,
    factor, inverse, diag, outs, updated, panel, abuf, acc, s1, r1, s2, r2, kept, moved, below, cs, cr, total, sums, gsum,
    in_sem, o_sem, a_sem, ring_s, ring_r, s1s, r1s, s2s, r2s, mov_s, mov_r, bel_s, bel_r, bel_l, cs_s, cs_r, ag_s, ag_r,
):
    chips, n, depth = dims
    supers, piece, block = factor.shape
    rows, pair = acc.shape[1], acc.shape[2]
    width = pair // 2
    chunks = supers * chips
    half = piece // 2
    tall = rows // TILES
    per_slab = rows // piece
    slabs = n // per_slab
    part = width // n
    r = lax.axis_index("row")
    c = lax.axis_index("col")
    x, k = r // 2, r % 2
    mate = x * 2 + 1 - k
    source_row = c // slabs
    source_x, source_k = source_row // 2, source_row % 2
    source = r == source_row
    passing = (k == source_k) & (x != source_x)
    home = x == source_x
    last = supers - 1
    length = n // depth
    steps = chunks * n

    def col_at(pos):
        y, i = pos // length, pos % length
        return (i + (y % 2) * (length - 1 - 2 * i)) * depth + y

    y, z = c % depth, c // depth
    pos = y * length + z + (y % 2) * (length - 1 - 2 * z)
    right, left = col_at((pos + 1) % n), col_at((pos + n - 1) % n)

    def src_of(j):
        t = (j + 1) // 2
        return col_at((pos + (1 - 2 * (j % 2)) * t + n) % n)

    def a_copy(i):
        src = src_of(i % n)
        if strips:
            view = a_ref.at[src]
        else:
            view = a_ref.at[:, pl.ds(pl.multiple_of(src * piece, piece), piece)]
        return pltpu.make_async_copy(view, abuf.at[i % DEEP], a_sem.at[i % DEEP])

    def block_of(g, at_x):
        return (at_x + 1 + g // supers) % chips

    def slot_of(g):
        return (g % supers) * chips + block_of(g, source_x)

    def ring(g, t, d, q, src):
        h = q + d - 2 * q * d
        view = panel.at[g, src, pl.ds(h * half, half)]
        return pltpu.make_async_remote_copy(
            src_ref=view, dst_ref=view,
            send_sem=ring_s.at[g], recv_sem=ring_r.at[d, g % 2, t - 1, q],
            device_id=(r, right * (1 - d) + left * d), device_id_type=MESH,
        )

    def coupled(s, first, count):
        low = order_ref[pl.ds(s, 1), 0:NSEL] * block
        label = first + lax.broadcasted_iota(jnp.int32, (count, NSEL), 0)
        return jnp.sum(jnp.where((label >= low) & (label < low + block), 1.0, 0.0), axis=1, keepdims=True)

    def norm(g, h):
        s = g % supers
        keep = coupled(s, (r * n + c) * piece + h * half, half)
        at = pl.ds(pl.multiple_of(block_of(g, x) * pair, pair), pair)
        term = jnp.dot(factor[s, h * half:(h + 1) * half, :], inverse[s, :, at], preferred_element_type=jnp.float32)
        panel[g, c, h * half:(h + 1) * half, :] = (term * keep).astype(jnp.bfloat16)

    def below_copy(slot, at, src, to_row, sem):
        return pltpu.make_async_remote_copy(
            src_ref=src, dst_ref=below.at[slot, at], send_sem=sem, recv_sem=bel_r.at[slot, at],
            device_id=(to_row, c), device_id_type=MESH,
        )

    def below_here(slot, at, g, src):
        return pltpu.make_async_copy(panel.at[g, src], below.at[slot, at], bel_l.at[slot])

    def lend(g, j):
        src = src_of(j)
        slot, at = slot_of(g), src % per_slab

        @pl.when(source & (src // per_slab == c % slabs))
        def _():
            below_copy(slot, at, panel.at[g, src], mate, bel_s.at[0]).start()
            below_here(slot, at, g, src).start()

    def lend_half(g, src, h):
        slot, at = slot_of(g), src % per_slab
        view = pl.ds(pl.multiple_of(h * half, half), half)

        @pl.when(source & (g % supers == last) & (src // per_slab == c % slabs))
        def _():
            for delta in range(1, chips):
                pltpu.make_async_remote_copy(
                    src_ref=panel.at[g, src, view], dst_ref=below.at[slot, at, view],
                    send_sem=bel_s.at[delta], recv_sem=bel_r.at[slot, at],
                    device_id=(((x + delta) % chips) * 2 + k, c), device_id_type=MESH,
                ).start()

    def pass_below(i):
        g, src = i // n, src_of(i % n)
        slot, at = slot_of(g), src % per_slab

        @pl.when(passing & (g % supers == last) & (src // per_slab == c % slabs))
        def _():
            copy = below_copy(slot, at, below.at[slot, at], mate, bel_s.at[0])
            copy.wait_recv()
            copy.start()

    def tile(m):
        return pl.ds(pl.multiple_of(m * tall, tall), tall)

    def mate_copy(g, m):
        return pltpu.make_async_remote_copy(
            src_ref=s1.at[g, tile(m)], dst_ref=r1.at[g, tile(m)],
            send_sem=s1s.at[0], recv_sem=r1s.at[g, m],
            device_id=(mate, c), device_id_type=MESH,
        )

    def cross_copy(g, m, slot):
        s = g % supers
        return pltpu.make_async_remote_copy(
            src_ref=s2.at[g, tile(m)], dst_ref=r2.at[s, slot, tile(m)],
            send_sem=s2s.at[0], recv_sem=r2s.at[s, slot],
            device_id=(block_of(g, x) * 2 + k, c), device_id_type=MESH,
        )

    def give(g, m):
        theirs = jnp.where(k == 0, acc[g % 2, tile(m), width:], acc[g % 2, tile(m), :width])
        s1[g, tile(m), :] = theirs.astype(jnp.bfloat16)
        mate_copy(g, m).start()

    def both(g, m):
        mate_copy(g, m).wait_recv()
        mine = jnp.where(k == 0, acc[g % 2, tile(m), :width], acc[g % 2, tile(m), width:])
        return mine + r1[g, tile(m), :].astype(jnp.float32)

    def send_across(g, m):
        s2[g, tile(m), :] = both(g, m).astype(jnp.bfloat16)
        cross_copy(g, m, x).start()

    def out_copy(s):
        return pltpu.make_async_copy(outs.at[s], out_hbm.at[s], o_sem.at[s])

    def cross_wait(s, slot):
        pltpu.make_async_remote_copy(
            src_ref=s2.at[0], dst_ref=r2.at[s, slot], send_sem=s2s.at[0], recv_sem=r2s.at[s, slot],
            device_id=(mate, c), device_id_type=MESH,
        ).wait_recv()

    def finish(g, s):
        for delta in range(1, chips):
            cross_wait(s, (x + delta) % chips)

        @pl.loop(0, TILES)
        def _(m):
            whole = both(g, m)
            for delta in range(1, chips):
                whole += r2[s, (x + delta) % chips, tile(m), :].astype(jnp.float32)
            outs[s, tile(m), :] = (-(whole * kept[s, tile(m), :])).astype(jnp.bfloat16)

    def move(s, slot):
        return pltpu.make_async_remote_copy(
            src_ref=outs.at[s], dst_ref=moved.at[s, slot], send_sem=mov_s.at[s], recv_sem=mov_r.at[s, slot],
            device_id=(source_x * 2 + k, c), device_id_type=MESH,
        )

    def piece_copy(s, first, count, slot, plane, to):
        return pltpu.make_async_remote_copy(
            src_ref=cs.at[s, pl.ds(first, count)], dst_ref=cr.at[s, pl.ds(slot, count)],
            send_sem=cs_s.at[s], recv_sem=cs_r.at[s],
            device_id=(plane * 2 + k, to), device_id_type=MESH,
        )

    def gather(s, slot, count, to):
        return pltpu.make_async_remote_copy(
            src_ref=total.at[s, pl.ds(0, count)], dst_ref=sums.at[s, pl.ds(slot, count)],
            send_sem=ag_s.at[s], recv_sem=ag_r.at[s],
            device_id=(r, to), device_id_type=MESH,
        )

    def below_wait(s):
        for e in range(chips):
            slot = slot_of(e * supers + s)

            @pl.when(source)
            def _():
                pltpu.make_async_copy(below.at[slot], below.at[slot], bel_l.at[slot]).wait()

    def correct(s, first, end, left_of):
        @pl.loop(first, end)
        def _(j):
            src = src_of(j)
            at = src % per_slab

            @pl.when(src // per_slab == c % slabs)
            def _():
                left = left_of(pl.ds(pl.multiple_of(at * piece, piece), piece))
                for b in range(chips):
                    gsum[:, b * pair:(b + 1) * pair] -= lax.dot_general(
                        left, below[s * chips + b, at], (((0,), (0,)), ((), ())), preferred_element_type=jnp.float32
                    )

    def below_arrived(s, first, end):
        @pl.loop(first, end)
        def _(j):
            src = src_of(j)
            at = src % per_slab

            @pl.when((k != source_k) & (src // per_slab == c % slabs))
            def _():
                for e in range(chips):
                    slot = slot_of(e * supers + s)
                    below_copy(slot, at, below.at[slot, at], mate, bel_s.at[0]).wait_recv()

    def fill(s, delta):
        for b in range(n):
            cs[s, delta * n + b] = gsum[b * part:(b + 1) * part, :].astype(jnp.bfloat16)
        if delta == 0:
            cr[s, c] = cs[s, c]

    def spread(s, delta):
        plane = (x + delta) % chips
        for ahead in range(0 if delta else 1, n):
            to = (c + ahead) % n
            piece_copy(s, delta * n + to, 1, c, plane, to).start()

    def early_own(s):
        @pl.when(home)
        def _():
            below_wait(s)
            below_arrived(s, 0, n)
            gsum[...] = jnp.zeros_like(gsum)
            correct(s, 0, n, lambda at: outs[s, at, :])
            fill(s, 0)

    def early_other(s):
        for delta in range(1, chips):
            plane = (x + delta) % chips
            move(s, plane).wait_recv()
            gsum[...] = jnp.zeros_like(gsum)
            correct(s, 0, n, lambda at: moved[s, plane, at, :])
            fill(s, delta)

    def early_send(s):
        @pl.when(home)
        def _():
            for delta in range(1, chips):
                spread(s, delta)

    def collect(s):
        if s == last:
            piece_copy(s, 0, n - 1, 0, x, c).wait_recv()
        else:
            @pl.when(home)
            def _():
                piece_copy(s, 0, n - 1, 0, x, c).wait_recv()

            @pl.when(x != source_x)
            def _():
                piece_copy(s, 0, n, 0, x, c).wait_recv()
        summed = cr[s, 0].astype(jnp.float32)
        for b in range(1, n):
            summed += cr[s, b].astype(jnp.float32)
        total[s, 0] = summed.astype(jnp.bfloat16)
        for ahead in range(1, n):
            gather(s, c, 1, (c + ahead) % n).start()
        sums[s, c] = summed.astype(jnp.bfloat16)

    def updated_copy(s):
        return pltpu.make_async_copy(updated.at[s], updated_hbm.at[s], o_sem.at[supers + s])

    def update(s):
        pltpu.make_async_remote_copy(
            src_ref=sums.at[s, pl.ds(0, n - 1)], dst_ref=sums.at[s, pl.ds(0, n - 1)],
            send_sem=ag_s.at[s], recv_sem=ag_r.at[s], device_id=(mate, c), device_id_type=MESH,
        ).wait_recv()
        for b in range(n):
            gsum[b * part:(b + 1) * part, :] = sums[s, b].astype(jnp.float32)
        updated[s] = diag[s] + gsum[...].T
        updated_copy(s).start()

    def factor_copy(s):
        return pltpu.make_async_copy(factor_hbm.at[s], factor.at[s], in_sem.at[s])

    def inverse_copy(s):
        return pltpu.make_async_copy(inverse_hbm.at[s], inverse.at[s], in_sem.at[supers + s])

    def sent(ref, sem):
        pltpu.make_async_remote_copy(
            src_ref=ref, dst_ref=ref, send_sem=sem, recv_sem=sem, device_id=(mate, c), device_id_type=MESH
        ).wait_send()

    def drain():
        for g in range(chunks):
            sent(panel.at[g, pl.ds(0, n - 1)], ring_s.at[g])
        sent(s1, s1s.at[0])
        sent(s2, s2s.at[0])
        ending = below.at[pl.ds(last * chips, chips)]

        @pl.when(source)
        def _():
            sent(below, bel_s.at[0])
            for delta in range(1, chips):
                sent(ending, bel_s.at[delta])

        @pl.when(passing)
        def _():
            sent(ending, bel_s.at[0])

        for s in range(last):
            @pl.when(x != source_x)
            def _():
                sent(outs.at[s], mov_s.at[s])

    def pieces_sent(s):
        if s == last:
            sent(cs.at[s, pl.ds(0, n - 1)], cs_s.at[s])
        else:
            @pl.when(home)
            def _():
                sent(cs.at[s, pl.ds(0, chips * n - 1)], cs_s.at[s])
        sent(sums.at[s, pl.ds(0, n - 1)], ag_s.at[s])

    diag_copy = pltpu.make_async_copy(diag_hbm, diag, in_sem.at[2 * supers])

    barrier = pltpu.get_barrier_semaphore()
    pl.semaphore_signal(barrier, inc=1, device_id=(mate, c), device_id_type=MESH)
    for delta in range(chips):
        for ahead in range(0 if delta else 1, n):
            there = (((x + delta) % chips) * 2 + k, (c + ahead) % n)
            pl.semaphore_signal(barrier, inc=1, device_id=there, device_id_type=MESH)
    for s in range(supers):
        factor_copy(s).start()
        inverse_copy(s).start()
    for i in range(DEEP - 1):
        a_copy(i).start()
    diag_copy.start()
    factor_copy(0).wait()
    inverse_copy(0).wait()
    norm(0, 0)
    pl.semaphore_wait(barrier, chips * n)
    ring(0, 1, 0, 0, c).start()
    norm(0, 1)
    ring(0, 1, 1, 0, c).start()
    for d in range(2):
        ring(0, 1, d, 1, c).start()
    for s in range(1, supers):
        factor_copy(s).wait()
        inverse_copy(s).wait()
    for g in range(1, chunks):
        for h in range(2):
            norm(g, h)
    for s in range(supers):
        @pl.loop(0, TILES)
        def _(m):
            kept[s, tile(m), :] = jnp.broadcast_to(coupled(s, c * rows + m * tall, tall), (tall, width))

    @pl.loop(0, steps)
    def _(i):
        g, j = i // n, i % n
        src = src_of(j)
        ahead, q = j // 2 + 1, j % 2

        @pl.when(ahead < n // 2)
        def _():
            for way in range(2):
                come = col_at((pos + (2 * way - 1) * ahead + n) % n)
                ring(g, ahead, way, q, come).wait_recv()

                @pl.when((ahead + 1 < n // 2) | (q == 0))
                def _():
                    ring(g, ahead + 1, way, q, come).start()

            for way in range(2):
                come = col_at((pos + (2 * way - 1) * ahead + n) % n)
                lend_half(g, come, q + way - 2 * q * way)

        @pl.when(((j == n - 4) | (j == n - 3)) & (g < chunks - 1))
        def _():
            for way in range(2):
                ring(g + 1, 1, way, q, c).start()

        @pl.when(j == n - 1)
        def _():
            for way in range(2):
                ring(g, n // 2, way, 0, src).wait_recv()
                lend_half(g, src, way)

        @pl.when(j == 0)
        def _():
            for h in range(2):
                lend_half(g, c, h)

        @pl.when((j == 0) | (j % 2 == 1))
        def _():
            lend(g, j)

        @pl.when((j < n - 1) & (j % 2 == 1))
        def _():
            lend(g, j + 1)

        @pl.when((i == steps - 1) & home)
        def _():
            for s in range(last):
                spread(s, 0)
                early_other(s)

        @pl.when((i >= LAG) & (i < steps - 2))
        def _():
            pass_below(i - LAG)

        @pl.when(i == steps - 2)
        def _():
            @pl.loop(steps - 2 - LAG, steps - 1 - NEAR)
            def _(late):
                pass_below(late)

        @pl.when(i == steps - 1)
        def _():
            pass_below(i - NEAR)

        a_copy(i).wait()

        @pl.when(i + DEEP - 1 < steps)
        def _():
            a_copy(i + DEEP - 1).start()

        @pl.loop(0, TILES)
        def _(m):
            term = jnp.dot(abuf[i % DEEP, tile(m), :], panel[g, src], preferred_element_type=jnp.float32)

            @pl.when(j == 0)
            def _():
                acc[g % 2, tile(m), :] = term

            @pl.when(j > 0)
            def _():
                acc[g % 2, tile(m), :] += term

            @pl.when(j == n - 1)
            def _():
                give(g, m)

        @pl.when((j >= BEGIN) & (j < BEGIN + TILES) & (g > 0) & (g <= chunks - supers))
        def _():
            send_across(g - 1, j - BEGIN)

        for s in range(last):
            own = chunks - supers + s

            @pl.when((j == 0) & (g == own + 1))
            def _():
                finish(own, s)
                out_copy(s).start()

                @pl.when(x != source_x)
                def _():
                    move(s, x).start()

            @pl.when((j == 3) & (g == own + 1))
            def _():
                early_own(s)
    for i in range(steps - NEAR, steps - 1):
        pass_below(i)
    finish(chunks - 1, last)
    out_copy(last).start()
    for s in range(last):
        early_send(s)
    gsum[...] = jnp.zeros_like(gsum)
    below_wait(last)
    below_arrived(last, 0, n - 1)
    correct(last, 0, n - 1, lambda at: outs[last, at, :])
    pass_below(steps - 1)
    below_arrived(last, n - 1, n)
    correct(last, n - 1, n, lambda at: outs[last, at, :])
    fill(last, 0)
    spread(last, 0)
    for s in range(last):
        collect(s)
    drain()
    diag_copy.wait()
    collect(last)
    for s in range(supers):
        update(s)
    for s in range(supers):
        pieces_sent(s)
    for s in range(supers):
        out_copy(s).wait()
        updated_copy(s).wait()


def body(ancestor_order, factor_rows, factor_inverse, ancestor_inverse, diagonal_inverse):
    supers, piece, block = factor_rows.shape
    rows = ancestor_inverse.shape[0]
    row_count, n = lax.axis_size("row"), lax.axis_size("col")
    chips = row_count // 2
    depth = chips
    width = block // row_count
    pair = 2 * width
    chunks = supers * chips

    strips = piece % 128 != 0
    left = ancestor_inverse
    if strips:
        left = left.reshape(rows, n, piece).transpose(1, 0, 2)
    per_slab = rows // piece
    part = width // n
    half_type, full_type, dma = jnp.bfloat16, jnp.float32, pltpu.SemaphoreType.DMA
    anywhere = pl.BlockSpec(memory_space=pl.ANY)
    return pl.pallas_call(
        functools.partial(kernel, (chips, n, depth), strips),
        out_shape=(
            jax.ShapeDtypeStruct((supers, rows, width), half_type),
            jax.ShapeDtypeStruct((supers, block, width), full_type),
        ),
        in_specs=[pl.BlockSpec(memory_space=pltpu.VMEM)] + [anywhere] * 4,
        out_specs=(anywhere,) * 2,
        scratch_shapes=[
            pltpu.VMEM((supers, piece, block), half_type),
            pltpu.VMEM((supers, block, block), half_type),
            pltpu.VMEM((supers, block, width), full_type),
            pltpu.VMEM((supers, rows, width), half_type),
            pltpu.VMEM((supers, block, width), full_type),
            pltpu.VMEM((chunks, n, piece, pair), half_type),
            pltpu.VMEM((DEEP, rows, piece), half_type),
            pltpu.VMEM((2, rows, pair), full_type),
            pltpu.VMEM((chunks, rows, width), half_type),
            pltpu.VMEM((chunks, rows, width), half_type),
            pltpu.VMEM((chunks - supers, rows, width), half_type),
            pltpu.VMEM((supers, chips, rows, width), half_type),
            pltpu.VMEM((supers, rows, width), full_type),
            pltpu.VMEM((max(supers - 1, 1), chips, rows, width), half_type),
            pltpu.VMEM((chunks, per_slab, piece, pair), half_type),
            pltpu.VMEM((supers, chips * n, part, block), half_type),
            pltpu.VMEM((supers, n, part, block), half_type),
            pltpu.VMEM((supers, 1, part, block), half_type),
            pltpu.VMEM((supers, n, part, block), half_type),
            pltpu.VMEM((width, block), full_type),
            dma((2 * supers + 1,)),
            dma((2 * supers,)),
            dma((DEEP,)),
            dma((chunks,)),
            dma((2, 2, n // 2, 2)),
            dma((1,)),
            dma((chunks, TILES)),
            dma((1,)),
            dma((supers, chips)),
            dma((max(supers - 1, 1),)),
            dma((max(supers - 1, 1), chips)),
            dma((chips,)),
            dma((chunks, per_slab)),
            dma((chunks,)),
            dma((supers,)),
            dma((supers,)),
            dma((supers,)),
            dma((supers,)),
        ],
        compiler_params=pltpu.CompilerParams(
            collective_id=0, has_side_effects=True, vmem_limit_bytes=64 * 1024 * 1024 - 65536
        ),
        cost_estimate=pl.CostEstimate(
            flops=2 * rows * n * piece * supers * block, bytes_accessed=8 * rows * n * piece, transcendentals=0
        ),
    )(ancestor_order, factor_rows, factor_inverse, diagonal_inverse, left)


def solution(mesh):
    placed = (P(), P(None, ("row", "col"), None), P(), P("col", "row"), P(None, None, "row"))
    return jax.shard_map(
        body,
        mesh=mesh,
        in_specs=placed,
        out_specs=(P(None, "col", "row"), P(None, None, "row")),
        check_vma=False,
    )
```

time: 164 us -> 153 us (0.933)
  Pallas kernels: 159 us -> 149 us
    pallas_call x1, Pallas kernels: 159 us -> 149 us  [body(): pl.pallas_call(functools.partial(kernel, (chips, n, depth), strips), out_...]
where the time goes in v2:
time: 153 us
  Pallas kernels  149 us (97%)
  local copies, waits for them, and re-layouts  3.51 us (2%)
    pallas_call x1, Pallas kernels, body(): pl.pallas_call(functools.partial(kernel, (chips, n, depth), strips), out_...  149 us
    unnamed x4, local copies, waits for them, and re-layouts  3.51 us

profile of v2, /device:TPU:1, one launch (start us, length us, event | category | flops | bytes accessed | tf_op | source)
XLA Modules:
  0.0 152.7 jit_solution(1672988913660853329)
XLA Ops:
  0.6 148.6 %shard_map.68 = (bf16[2,3072,128]{2,1,0:T(8,128)(2,1)}, f32[2,512,128]{2,1,0:T(8,128)}) custom-call(s32[2,48]{1,0:T(2,128)} %order_ref.1, bf16[2,768,512]{2,1,0:T(8,128)(2,1)} %factor_hbm.1, bf16[2,512,512]{2,1,0:T(8,128)(2,1)} %inverse_hbm.1, f32[2,512,128]{2,1,0:T(8,128)} %diag_hbm.1, bf16[3072,6144]{1,0:T(8,128)(2,1)} %a_ref.1), custom_call_target="tpu_custom_call" | custom-call | flops 38654705664 | bytes 150994944 | tf_op jit(solution)/shard_map/pallas_call | solution.py:536
  149.2 0.0 copy-start
  149.2 2.7 %copy.9 = bf16[2,3072,128]{2,1,0:T(8,128)(2,1)} copy(bf16[2,3072,128]{2,1,0:T(8,128)(2,1)} %get-tuple-element.4) | data formatting | bytes 3145728
  151.9 0.0 copy-done
  151.9 0.8 copy.10
Async XLA Ops:
  149.2 2.7 %copy-start = (f32[2,512,128]{2,1,0:T(8,128)S(1)}, f32[2,512,128]{2,1,0:T(8,128)}, u32[]{:S(2)}) copy-start(f32[2,512,128]{2,1,0:T(8,128)} %get-tuple-element.5) | copy-start | bytes 1572868

commit v3 on v2

--- a/solution.py
+++ b/solution.py
@@ -17,9 +17,9 @@
 
 
 def kernel(
-    dims, strips, order_ref, factor_hbm, inverse_hbm, diag_hbm, a_ref, out_hbm, updated_hbm,
-    factor, inverse, diag, outs, updated, panel, abuf, acc, s1, r1, s2, r2, kept, moved, below, cs, cr, total, sums, gsum,
-    in_sem, o_sem, a_sem, ring_s, ring_r, s1s, r1s, s2s, r2s, mov_s, mov_r, bel_s, bel_r, bel_l, cs_s, cs_r, ag_s, ag_r,
+    dims, strips, order_ref, factor_hbm, inverse_hbm, diag_hbm, a_ref, outs, updated,
+    factor, inverse, diag, panel, abuf, acc, s1, r1, s2, r2, kept, moved, below, cs, cr, total, sums, gsum,
+    in_sem, a_sem, ring_s, ring_r, s1s, r1s, s2s, r2s, mov_s, mov_r, bel_s, bel_r, bel_l, cs_s, cs_r, ag_s, ag_r,
 ):
     chips, n, depth = dims
     supers, piece, block = factor.shape
@@ -164,9 +164,6 @@
         s2[g, tile(m), :] = both(g, m).astype(jnp.bfloat16)
         cross_copy(g, m, x).start()
 
-    def out_copy(s):
-        return pltpu.make_async_copy(outs.at[s], out_hbm.at[s], o_sem.at[s])
-
     def cross_wait(s, slot):
         pltpu.make_async_remote_copy(
             src_ref=s2.at[0], dst_ref=r2.at[s, slot], send_sem=s2s.at[0], recv_sem=r2s.at[s, slot],
@@ -238,6 +235,16 @@
                     slot = slot_of(e * supers + s)
                     below_copy(slot, at, below.at[slot, at], mate, bel_s.at[0]).wait_recv()
 
+    def farthest_first(send):
+        for i in range(length):
+            there = jnp.where(2 * z < length, length - 1 - i, i)
+            for u in range(depth):
+                to = there * depth + (y + 1 + u) % depth
+
+                @pl.when(to != c)
+                def _():
+                    send(to)
+
     def fill(s, delta):
         for b in range(n):
             cs[s, delta * n + b] = gsum[b * part:(b + 1) * part, :].astype(jnp.bfloat16)
@@ -246,9 +253,13 @@
 
     def spread(s, delta):
         plane = (x + delta) % chips
-        for ahead in range(0 if delta else 1, n):
-            to = (c + ahead) % n
+
+        def send(to):
             piece_copy(s, delta * n + to, 1, c, plane, to).start()
+
+        if delta:
+            send(c)
+        farthest_first(send)
 
     def early_own(s):
         @pl.when(home)
@@ -288,12 +299,8 @@
         for b in range(1, n):
             summed += cr[s, b].astype(jnp.float32)
         total[s, 0] = summed.astype(jnp.bfloat16)
-        for ahead in range(1, n):
-            gather(s, c, 1, (c + ahead) % n).start()
+        farthest_first(lambda to: gather(s, c, 1, to).start())
         sums[s, c] = summed.astype(jnp.bfloat16)
-
-    def updated_copy(s):
-        return pltpu.make_async_copy(updated.at[s], updated_hbm.at[s], o_sem.at[supers + s])
 
     def update(s):
         pltpu.make_async_remote_copy(
@@ -303,7 +310,6 @@
         for b in range(n):
             gsum[b * part:(b + 1) * part, :] = sums[s, b].astype(jnp.float32)
         updated[s] = diag[s] + gsum[...].T
-        updated_copy(s).start()
 
     def factor_copy(s):
         return pltpu.make_async_copy(factor_hbm.at[s], factor.at[s], in_sem.at[s])
@@ -351,10 +357,10 @@
 
     barrier = pltpu.get_barrier_semaphore()
     pl.semaphore_signal(barrier, inc=1, device_id=(mate, c), device_id_type=MESH)
-    for delta in range(chips):
-        for ahead in range(0 if delta else 1, n):
-            there = (((x + delta) % chips) * 2 + k, (c + ahead) % n)
-            pl.semaphore_signal(barrier, inc=1, device_id=there, device_id_type=MESH)
+    for near in (right, left):
+        pl.semaphore_signal(barrier, inc=1, device_id=(r, near), device_id_type=MESH)
+    for delta in range(1, chips):
+        pl.semaphore_signal(barrier, inc=1, device_id=(((x + delta) % chips) * 2 + k, c), device_id_type=MESH)
     for s in range(supers):
         factor_copy(s).start()
         inverse_copy(s).start()
@@ -364,7 +370,7 @@
     factor_copy(0).wait()
     inverse_copy(0).wait()
     norm(0, 0)
-    pl.semaphore_wait(barrier, chips * n)
+    pl.semaphore_wait(barrier, chips + 2)
     ring(0, 1, 0, 0, c).start()
     norm(0, 1)
     ring(0, 1, 1, 0, c).start()
@@ -477,7 +483,6 @@
             @pl.when((j == 0) & (g == own + 1))
             def _():
                 finish(own, s)
-                out_copy(s).start()
 
                 @pl.when(x != source_x)
                 def _():
@@ -489,7 +494,6 @@
     for i in range(steps - NEAR, steps - 1):
         pass_below(i)
     finish(chunks - 1, last)
-    out_copy(last).start()
     for s in range(last):
         early_send(s)
     gsum[...] = jnp.zeros_like(gsum)
@@ -510,9 +514,6 @@
         update(s)
     for s in range(supers):
         pieces_sent(s)
-    for s in range(supers):
-        out_copy(s).wait()
-        updated_copy(s).wait()
 
 
 def body(ancestor_order, factor_rows, factor_inverse, ancestor_inverse, diagonal_inverse):
@@ -536,16 +537,14 @@
     return pl.pallas_call(
         functools.partial(kernel, (chips, n, depth), strips),
         out_shape=(
-            jax.ShapeDtypeStruct((supers, rows, width), half_type),
-            jax.ShapeDtypeStruct((supers, block, width), full_type),
+            pltpu.VMEM((supers, rows, width), half_type),
+            pltpu.VMEM((supers, block, width), full_type),
         ),
         in_specs=[pl.BlockSpec(memory_space=pltpu.VMEM)] + [anywhere] * 4,
-        out_specs=(anywhere,) * 2,
+        out_specs=(pl.BlockSpec(memory_space=pltpu.VMEM),) * 2,
         scratch_shapes=[
             pltpu.VMEM((supers, piece, block), half_type),
             pltpu.VMEM((supers, block, block), half_type),
-            pltpu.VMEM((supers, block, width), full_type),
-            pltpu.VMEM((supers, rows, width), half_type),
             pltpu.VMEM((supers, block, width), full_type),
             pltpu.VMEM((chunks, n, piece, pair), half_type),
             pltpu.VMEM((DEEP, rows, piece), half_type),
@@ -563,7 +562,6 @@
             pltpu.VMEM((supers, n, part, block), half_type),
             pltpu.VMEM((width, block), full_type),
             dma((2 * supers + 1,)),
-            dma((2 * supers,)),
             dma((DEEP,)),
             dma((chunks,)),
             dma((2, 2, n // 2, 2)),
@@ -582,7 +580,7 @@
             dma((supers,)),
         ],
         compiler_params=pltpu.CompilerParams(
-            collective_id=0, has_side_effects=True, vmem_limit_bytes=64 * 1024 * 1024 - 65536
+            collective_id=0, has_side_effects=True, vmem_limit_bytes=61 * 1024 * 1024
         ),
         cost_estimate=pl.CostEstimate(
             flops=2 * rows * n * piece * supers * block, bytes_accessed=8 * rows * n * piece, transcendentals=0

time: 153 us -> 148 us (0.967)
  Pallas kernels: 149 us -> 145 us
  local copies, waits for them, and re-layouts: 3.51 us -> 1.94 us
    pallas_call x1, Pallas kernels: 149 us -> 145 us  [body(): pl.pallas_call(functools.partial(kernel, (chips, n, depth), strips), out_...]
    unnamed x4 -> x2, local copies, waits for them, and re-layouts: 3.51 us -> 1.94 us
where the time goes in v3:
time: 148 us
  Pallas kernels  145 us (98%)
  local copies, waits for them, and re-layouts  1.94 us (1%)
    pallas_call x1, Pallas kernels, body(): pl.pallas_call(functools.partial(kernel, (chips, n, depth), strips), out_...  145 us

profile of v3, /device:TPU:1, one launch (start us, length us, event | category | flops | bytes accessed | tf_op | source)
XLA Modules:
  0.0 147.6 jit_solution(13485852454861656256)
XLA Ops:
  0.6 145.0 %shard_map.68 = (bf16[2,3072,128]{2,1,0:T(8,128)(2,1)S(1)}, f32[2,512,128]{2,1,0:T(8,128)S(1)}) custom-call(s32[2,48]{1,0:T(2,128)} %order_ref.1, bf16[2,768,512]{2,1,0:T(8,128)(2,1)} %factor_hbm.1, bf16[2,512,512]{2,1,0:T(8,128)(2,1)} %inverse_hbm.1, f32[2,512,128]{2,1,0:T(8,128)} %diag_hbm.1, bf16[3072,6144]{1,0:T(8,128)(2,1)} %a_ref.1), custom_call_target="tpu_custom_call" | custom-call | flops 38654705664 | bytes 150994944 | tf_op jit(solution)/shard_map/pallas_call | solution.py:537
  145.6 1.1 copy.9
  146.8 0.8 copy.10

commit v4 on v3

--- a/solution.py
+++ b/solution.py
@@ -27,6 +27,7 @@
     width = pair // 2
     chunks = supers * chips
     half = piece // 2
+    cut = -(-half // 32) * 16
     tall = rows // TILES
     per_slab = rows // piece
     slabs = n // per_slab
@@ -79,6 +80,17 @@
             device_id=(r, right * (1 - d) + left * d), device_id_type=MESH,
         )
 
+    def ring_end(g, d, q, src):
+        view = panel.at[g, src, pl.ds(end_at(d, q), (cut, half - cut)[q])]
+        return pltpu.make_async_remote_copy(
+            src_ref=view, dst_ref=view,
+            send_sem=ring_s.at[g], recv_sem=ring_r.at[d, g % 2, n // 2 - 1, q],
+            device_id=(r, right * (1 - d) + left * d), device_id_type=MESH,
+        )
+
+    def end_at(d, q):
+        return d * half + q * cut
+
     def coupled(s, first, count):
         low = order_ref[pl.ds(s, 1), 0:NSEL] * block
         label = first + lax.broadcasted_iota(jnp.int32, (count, NSEL), 0)
@@ -109,9 +121,9 @@
             below_copy(slot, at, panel.at[g, src], mate, bel_s.at[0]).start()
             below_here(slot, at, g, src).start()
 
-    def lend_half(g, src, h):
+    def lend_part(g, src, first, count):
         slot, at = slot_of(g), src % per_slab
-        view = pl.ds(pl.multiple_of(h * half, half), half)
+        view = pl.ds(first, count)
 
         @pl.when(source & (g % supers == last) & (src // per_slab == c % slabs))
         def _():
@@ -170,16 +182,19 @@
             device_id=(mate, c), device_id_type=MESH,
         ).wait_recv()
 
+    def finish_tile(g, s, m):
+        whole = both(g, m)
+        for delta in range(1, chips):
+            whole += r2[s, (x + delta) % chips, tile(m), :].astype(jnp.float32)
+        outs[s, tile(m), :] = (-(whole * kept[s, tile(m), :])).astype(jnp.bfloat16)
+
     def finish(g, s):
         for delta in range(1, chips):
             cross_wait(s, (x + delta) % chips)
 
         @pl.loop(0, TILES)
         def _(m):
-            whole = both(g, m)
-            for delta in range(1, chips):
-                whole += r2[s, (x + delta) % chips, tile(m), :].astype(jnp.float32)
-            outs[s, tile(m), :] = (-(whole * kept[s, tile(m), :])).astype(jnp.bfloat16)
+            finish_tile(g, s, m)
 
     def move(s, slot):
         return pltpu.make_async_remote_copy(
@@ -209,31 +224,50 @@
             def _():
                 pltpu.make_async_copy(below.at[slot], below.at[slot], bel_l.at[slot]).wait()
 
-    def correct(s, first, end, left_of):
-        @pl.loop(first, end)
-        def _(j):
-            src = src_of(j)
-            at = src % per_slab
-
-            @pl.when(src // per_slab == c % slabs)
-            def _():
-                left = left_of(pl.ds(pl.multiple_of(at * piece, piece), piece))
-                for b in range(chips):
-                    gsum[:, b * pair:(b + 1) * pair] -= lax.dot_general(
-                        left, below[s * chips + b, at], (((0,), (0,)), ((), ())), preferred_element_type=jnp.float32
-                    )
-
-    def below_arrived(s, first, end):
-        @pl.loop(first, end)
-        def _(j):
-            src = src_of(j)
-            at = src % per_slab
-
-            @pl.when((k != source_k) & (src // per_slab == c % slabs))
-            def _():
-                for e in range(chips):
-                    slot = slot_of(e * supers + s)
-                    below_copy(slot, at, below.at[slot, at], mate, bel_s.at[0]).wait_recv()
+    def correct(s, at, left_of):
+        left = left_of(pl.ds(pl.multiple_of(at * piece, piece), piece))
+        for b in range(chips):
+            gsum[:, b * pair:(b + 1) * pair] -= lax.dot_general(
+                left, below[s * chips + b, at], (((0,), (0,)), ((), ())), preferred_element_type=jnp.float32
+            )
+
+    def correct_all(s, left_of):
+        @pl.loop(0, per_slab)
+        def _(at):
+            correct(s, at, left_of)
+
+    def below_arrived(s, at):
+        @pl.when(k != source_k)
+        def _():
+            for e in range(chips):
+                slot = slot_of(e * supers + s)
+                below_copy(slot, at, below.at[slot, at], mate, bel_s.at[0]).wait_recv()
+
+    def finish_last():
+        far = src_of(n - 1)
+        own_far = far // per_slab == c % slabs
+        per_tile = per_slab // TILES
+        for delta in range(1, chips):
+            cross_wait(last, (x + delta) % chips)
+        below_wait(last)
+
+        @pl.loop(0, TILES)
+        def _(m):
+            finish_tile(chunks - 1, last, m)
+
+            @pl.loop(m * per_tile, (m + 1) * per_tile)
+            def _(at):
+                @pl.when((x == source_x) | (far // per_slab != c % slabs) | (at != far % per_slab))
+                def _():
+                    below_arrived(last, at)
+                    correct(last, at, lambda rows_at: outs[last, rows_at, :])
+
+        pass_below(steps - 1)
+
+        @pl.when((x != source_x) & own_far)
+        def _():
+            below_arrived(last, far % per_slab)
+            correct(last, far % per_slab, lambda rows_at: outs[last, rows_at, :])
 
     def farthest_first(send):
         for i in range(length):
@@ -265,9 +299,10 @@
         @pl.when(home)
         def _():
             below_wait(s)
-            below_arrived(s, 0, n)
+            for at in range(per_slab):
+                below_arrived(s, at)
             gsum[...] = jnp.zeros_like(gsum)
-            correct(s, 0, n, lambda at: outs[s, at, :])
+            correct_all(s, lambda at: outs[s, at, :])
             fill(s, 0)
 
     def early_other(s):
@@ -275,7 +310,7 @@
             plane = (x + delta) % chips
             move(s, plane).wait_recv()
             gsum[...] = jnp.zeros_like(gsum)
-            correct(s, 0, n, lambda at: moved[s, plane, at, :])
+            correct_all(s, lambda at: moved[s, plane, at, :])
             fill(s, delta)
 
     def early_send(s):
@@ -355,18 +390,14 @@
 
     diag_copy = pltpu.make_async_copy(diag_hbm, diag, in_sem.at[2 * supers])
 
+    factor_copy(0).start()
+    inverse_copy(0).start()
     barrier = pltpu.get_barrier_semaphore()
-    pl.semaphore_signal(barrier, inc=1, device_id=(mate, c), device_id_type=MESH)
     for near in (right, left):
         pl.semaphore_signal(barrier, inc=1, device_id=(r, near), device_id_type=MESH)
+    pl.semaphore_signal(barrier, inc=1, device_id=(mate, c), device_id_type=MESH)
     for delta in range(1, chips):
         pl.semaphore_signal(barrier, inc=1, device_id=(((x + delta) % chips) * 2 + k, c), device_id_type=MESH)
-    for s in range(supers):
-        factor_copy(s).start()
-        inverse_copy(s).start()
-    for i in range(DEEP - 1):
-        a_copy(i).start()
-    diag_copy.start()
     factor_copy(0).wait()
     inverse_copy(0).wait()
     norm(0, 0)
@@ -377,6 +408,12 @@
     for d in range(2):
         ring(0, 1, d, 1, c).start()
     for s in range(1, supers):
+        factor_copy(s).start()
+        inverse_copy(s).start()
+    for i in range(DEEP - 1):
+        a_copy(i).start()
+    diag_copy.start()
+    for s in range(1, supers):
         factor_copy(s).wait()
         inverse_copy(s).wait()
     for g in range(1, chunks):
@@ -399,29 +436,36 @@
                 come = col_at((pos + (2 * way - 1) * ahead + n) % n)
                 ring(g, ahead, way, q, come).wait_recv()
 
-                @pl.when((ahead + 1 < n // 2) | (q == 0))
+                @pl.when(ahead + 1 < n // 2)
                 def _():
                     ring(g, ahead + 1, way, q, come).start()
 
+                @pl.when((ahead + 1 == n // 2) & (q == 0))
+                def _():
+                    for e in range(2):
+                        ring_end(g, way, e, come).start()
+
             for way in range(2):
                 come = col_at((pos + (2 * way - 1) * ahead + n) % n)
-                lend_half(g, come, q + way - 2 * q * way)
+                lend_part(g, come, pl.multiple_of((q + way - 2 * q * way) * half, half), half)
 
         @pl.when(((j == n - 4) | (j == n - 3)) & (g < chunks - 1))
         def _():
             for way in range(2):
                 ring(g + 1, 1, way, q, c).start()
 
-        @pl.when(j == n - 1)
-        def _():
-            for way in range(2):
-                ring(g, n // 2, way, 0, src).wait_recv()
-                lend_half(g, src, way)
+        far = src_of(n - 1)
+        for e in range(2):
+            @pl.when(j == n - 2 + e)
+            def _():
+                for way in range(2):
+                    ring_end(g, way, e, far).wait_recv()
+                    lend_part(g, far, end_at(way, e), (cut, half - cut)[e])
 
         @pl.when(j == 0)
         def _():
             for h in range(2):
-                lend_half(g, c, h)
+                lend_part(g, c, h * half, half)
 
         @pl.when((j == 0) | (j % 2 == 1))
         def _():
@@ -436,6 +480,7 @@
             for s in range(last):
                 spread(s, 0)
                 early_other(s)
+                early_send(s)
 
         @pl.when((i >= LAG) & (i < steps - 2))
         def _():
@@ -493,16 +538,8 @@
                 early_own(s)
     for i in range(steps - NEAR, steps - 1):
         pass_below(i)
-    finish(chunks - 1, last)
-    for s in range(last):
-        early_send(s)
     gsum[...] = jnp.zeros_like(gsum)
-    below_wait(last)
-    below_arrived(last, 0, n - 1)
-    correct(last, 0, n - 1, lambda at: outs[last, at, :])
-    pass_below(steps - 1)
-    below_arrived(last, n - 1, n)
-    correct(last, n - 1, n, lambda at: outs[last, at, :])
+    finish_last()
     fill(last, 0)
     spread(last, 0)
     for s in range(last):
@@ -516,6 +553,14 @@
         pieces_sent(s)
 
 
+def store(outs, updated, out_hbm, updated_hbm, sem):
+    copies = [pltpu.make_async_copy(a, b, sem.at[i]) for i, (a, b) in enumerate(((outs, out_hbm), (updated, updated_hbm)))]
+    for copy in copies:
+        copy.start()
+    for copy in copies:
+        copy.wait()
+
+
 def body(ancestor_order, factor_rows, factor_inverse, ancestor_inverse, diagonal_inverse):
     supers, piece, block = factor_rows.shape
     rows = ancestor_inverse.shape[0]
@@ -534,7 +579,11 @@
     part = width // n
     half_type, full_type, dma = jnp.bfloat16, jnp.float32, pltpu.SemaphoreType.DMA
     anywhere = pl.BlockSpec(memory_space=pl.ANY)
-    return pl.pallas_call(
+    shapes = (
+        jax.ShapeDtypeStruct((supers, rows, width), half_type),
+        jax.ShapeDtypeStruct((supers, block, width), full_type),
+    )
+    found = pl.pallas_call(
         functools.partial(kernel, (chips, n, depth), strips),
         out_shape=(
             pltpu.VMEM((supers, rows, width), half_type),
@@ -586,6 +635,14 @@
             flops=2 * rows * n * piece * supers * block, bytes_accessed=8 * rows * n * piece, transcendentals=0
         ),
     )(ancestor_order, factor_rows, factor_inverse, diagonal_inverse, left)
+    return pl.pallas_call(
+        store,
+        out_shape=shapes,
+        in_specs=[pl.BlockSpec(memory_space=pltpu.VMEM)] * 2,
+        out_specs=(anywhere,) * 2,
+        scratch_shapes=[dma((2,))],
+        compiler_params=pltpu.CompilerParams(vmem_limit_bytes=1024 * 1024),
+    )(*(pltpu.with_memory_space_constraint(one, pltpu.VMEM) for one in found))
 
 
 def solution(mesh):

time: 148 us -> 146 us (0.986)
  local copies, waits for them, and re-layouts: 1.94 us -> 0 us
    unnamed x2 -> x0, local copies, waits for them, and re-layouts: 1.94 us -> none
where the time goes in v4:
time: 146 us
  Pallas kernels  146 us (100%)
    pallas_call x1, Pallas kernels, body(): pl.pallas_call(functools.partial(kernel, (chips, n, depth), strips), out_...  144 us

profile of v4, /device:TPU:1, one launch (start us, length us, event | category | flops | bytes accessed | tf_op | source)
XLA Modules:
  0.0 146.2 jit_solution(17569279329306358506)
XLA Ops:
  0.6 144.2 %shard_map.68 = (bf16[2,3072,128]{2,1,0:T(8,128)(2,1)S(1)}, f32[2,512,128]{2,1,0:T(8,128)S(1)}) custom-call(s32[2,48]{1,0:T(2,128)} %order_ref.1, bf16[2,768,512]{2,1,0:T(8,128)(2,1)} %factor_hbm.1, bf16[2,512,512]{2,1,0:T(8,128)(2,1)} %inverse_hbm.1, f32[2,512,128]{2,1,0:T(8,128)} %diag_hbm.1, bf16[3072,6144]{1,0:T(8,128)(2,1)} %a_ref.1), custom_call_target="tpu_custom_call" | custom-call | flops 38654705664 | bytes 150994944 | tf_op jit(solution)/shard_map/pallas_call | solution.py:586
  144.9 1.3 shard_map.69

commit v5 on v4

--- a/solution.py
+++ b/solution.py
@@ -17,8 +17,8 @@
 
 
 def kernel(
-    dims, strips, order_ref, factor_hbm, inverse_hbm, diag_hbm, a_ref, outs, updated,
-    factor, inverse, diag, panel, abuf, acc, s1, r1, s2, r2, kept, moved, below, cs, cr, total, sums, gsum,
+    dims, strips, order_hbm, factor_hbm, inverse_hbm, diag_hbm, a_ref, outs, updated,
+    order_ref, factor, inverse, diag, panel, abuf, acc, s1, r1, s2, r2, kept, moved, below, cs, cr, total, sums, gsum,
     in_sem, a_sem, ring_s, ring_r, s1s, r1s, s2s, r2s, mov_s, mov_r, bel_s, bel_r, bel_l, cs_s, cs_r, ag_s, ag_r,
 ):
     chips, n, depth = dims
@@ -76,7 +76,7 @@
         view = panel.at[g, src, pl.ds(h * half, half)]
         return pltpu.make_async_remote_copy(
             src_ref=view, dst_ref=view,
-            send_sem=ring_s.at[g], recv_sem=ring_r.at[d, g % 2, t - 1, q],
+            send_sem=ring_s.at[g], recv_sem=ring_r.at[d, t - 1, q],
             device_id=(r, right * (1 - d) + left * d), device_id_type=MESH,
         )
 
@@ -84,7 +84,7 @@
         view = panel.at[g, src, pl.ds(end_at(d, q), (cut, half - cut)[q])]
         return pltpu.make_async_remote_copy(
             src_ref=view, dst_ref=view,
-            send_sem=ring_s.at[g], recv_sem=ring_r.at[d, g % 2, n // 2 - 1, q],
+            send_sem=ring_s.at[g], recv_sem=ring_r.at[d, n // 2 - 1, q],
             device_id=(r, right * (1 - d) + left * d), device_id_type=MESH,
         )
 
@@ -349,6 +349,16 @@
     def factor_copy(s):
         return pltpu.make_async_copy(factor_hbm.at[s], factor.at[s], in_sem.at[s])
 
+    def first_factor(h):
+        at = pl.ds(h * half, half)
+        return pltpu.make_async_copy(factor_hbm.at[0, at], factor.at[0, at], in_sem.at[h * supers])
+
+    def first_inverse(e):
+        columns = pl.ds(pl.multiple_of(block_of(e * supers, x) * pair, pair), pair)
+        return pltpu.make_async_copy(
+            inverse_hbm.at[0, :, columns], inverse.at[0, :, columns], in_sem.at[2 * supers + 2 + e]
+        )
+
     def inverse_copy(s):
         return pltpu.make_async_copy(inverse_hbm.at[s], inverse.at[s], in_sem.at[supers + s])
 
@@ -388,31 +398,41 @@
                 sent(cs.at[s, pl.ds(0, chips * n - 1)], cs_s.at[s])
         sent(sums.at[s, pl.ds(0, n - 1)], ag_s.at[s])
 
+    order_copy = pltpu.make_async_copy(order_hbm, order_ref, in_sem.at[2 * supers + 1])
     diag_copy = pltpu.make_async_copy(diag_hbm, diag, in_sem.at[2 * supers])
 
-    factor_copy(0).start()
-    inverse_copy(0).start()
+    for h in range(2):
+        first_factor(h).start()
+        if h == 0:
+            first_inverse(0).start()
+            order_copy.start()
     barrier = pltpu.get_barrier_semaphore()
     for near in (right, left):
         pl.semaphore_signal(barrier, inc=1, device_id=(r, near), device_id_type=MESH)
     pl.semaphore_signal(barrier, inc=1, device_id=(mate, c), device_id_type=MESH)
     for delta in range(1, chips):
         pl.semaphore_signal(barrier, inc=1, device_id=(((x + delta) % chips) * 2 + k, c), device_id_type=MESH)
-    factor_copy(0).wait()
-    inverse_copy(0).wait()
+    order_copy.wait()
+    first_factor(0).wait()
+    first_inverse(0).wait()
     norm(0, 0)
     pl.semaphore_wait(barrier, chips + 2)
     ring(0, 1, 0, 0, c).start()
+    first_factor(1).wait()
     norm(0, 1)
     ring(0, 1, 1, 0, c).start()
     for d in range(2):
         ring(0, 1, d, 1, c).start()
+    for e in range(1, chips):
+        first_inverse(e).start()
     for s in range(1, supers):
         factor_copy(s).start()
         inverse_copy(s).start()
     for i in range(DEEP - 1):
         a_copy(i).start()
     diag_copy.start()
+    for e in range(1, chips):
+        first_inverse(e).wait()
     for s in range(1, supers):
         factor_copy(s).wait()
         inverse_copy(s).wait()
@@ -479,8 +499,6 @@
         def _():
             for s in range(last):
                 spread(s, 0)
-                early_other(s)
-                early_send(s)
 
         @pl.when((i >= LAG) & (i < steps - 2))
         def _():
@@ -538,6 +556,12 @@
                 early_own(s)
     for i in range(steps - NEAR, steps - 1):
         pass_below(i)
+    @pl.when(home)
+    def _():
+        for s in range(last):
+            early_other(s)
+            early_send(s)
+
     gsum[...] = jnp.zeros_like(gsum)
     finish_last()
     fill(last, 0)
@@ -589,9 +613,10 @@
             pltpu.VMEM((supers, rows, width), half_type),
             pltpu.VMEM((supers, block, width), full_type),
         ),
-        in_specs=[pl.BlockSpec(memory_space=pltpu.VMEM)] + [anywhere] * 4,
+        in_specs=[anywhere] * 5,
         out_specs=(pl.BlockSpec(memory_space=pltpu.VMEM),) * 2,
         scratch_shapes=[
+            pltpu.VMEM(ancestor_order.shape, ancestor_order.dtype),
             pltpu.VMEM((supers, piece, block), half_type),
             pltpu.VMEM((supers, block, block), half_type),
             pltpu.VMEM((supers, block, width), full_type),
@@ -610,10 +635,10 @@
             pltpu.VMEM((supers, 1, part, block), half_type),
             pltpu.VMEM((supers, n, part, block), half_type),
             pltpu.VMEM((width, block), full_type),
-            dma((2 * supers + 1,)),
+            dma((2 * supers + 2 + chips,)),
             dma((DEEP,)),
             dma((chunks,)),
-            dma((2, 2, n // 2, 2)),
+            dma((2, n // 2, 2)),
             dma((1,)),
             dma((chunks, TILES)),
             dma((1,)),

time: 146 us -> 145 us (level)
  Pallas kernels: 146 us -> 144 us
    pallas_call x1, Pallas kernels: 144 us -> 143 us  [body(): pl.pallas_call(functools.partial(kernel, (chips, n, depth), strips), out_...]
where the time goes in v5:
time: 145 us
  Pallas kernels  144 us (99%)
    pallas_call x1, Pallas kernels, body(): pl.pallas_call(functools.partial(kernel, (chips, n, depth), strips), out_...  143 us

profile of v5, /device:TPU:1, one launch (start us, length us, event | category | flops | bytes accessed | tf_op | source)
XLA Modules:
  0.0 144.6 jit_solution(3259322353310672897)
XLA Ops:
  0.6 142.6 %shard_map.68 = (bf16[2,3072,128]{2,1,0:T(8,128)(2,1)S(1)}, f32[2,512,128]{2,1,0:T(8,128)S(1)}) custom-call(s32[2,48]{1,0:T(2,128)} %order_hbm.1, bf16[2,768,512]{2,1,0:T(8,128)(2,1)} %factor_hbm.1, bf16[2,512,512]{2,1,0:T(8,128)(2,1)} %inverse_hbm.1, f32[2,512,128]{2,1,0:T(8,128)} %diag_hbm.1, bf16[3072,6144]{1,0:T(8,128)(2,1)} %a_ref.1), custom_call_target="tpu_custom_call" | custom-call | flops 38654705664 | bytes 150994944 | tf_op jit(solution)/shard_map/pallas_call | solution.py:610
  143.2 1.3 shard_map.69

commit v6 on v5

--- a/solution.py
+++ b/solution.py
@@ -19,7 +19,7 @@
 def kernel(
     dims, strips, order_hbm, factor_hbm, inverse_hbm, diag_hbm, a_ref, outs, updated,
     order_ref, factor, inverse, diag, panel, abuf, acc, s1, r1, s2, r2, kept, moved, below, cs, cr, total, sums, gsum,
-    in_sem, a_sem, ring_s, ring_r, s1s, r1s, s2s, r2s, mov_s, mov_r, bel_s, bel_r, bel_l, cs_s, cs_r, ag_s, ag_r,
+    in_sem, a_sem, ring_s, ring_r, s1s, r1s, s2s, r2s, mov_s, mov_r, bel_s, bel_r, bel_e, bel_l, cs_s, cs_r, ag_s, ag_r,
 ):
     chips, n, depth = dims
     supers, piece, block = factor.shape
@@ -121,16 +121,17 @@
             below_copy(slot, at, panel.at[g, src], mate, bel_s.at[0]).start()
             below_here(slot, at, g, src).start()
 
-    def lend_part(g, src, first, count):
+    def lend_part(g, src, first, count, sem=None):
         slot, at = slot_of(g), src % per_slab
         view = pl.ds(first, count)
+        sem = bel_r.at[slot, at] if sem is None else sem
 
         @pl.when(source & (g % supers == last) & (src // per_slab == c % slabs))
         def _():
             for delta in range(1, chips):
                 pltpu.make_async_remote_copy(
                     src_ref=panel.at[g, src, view], dst_ref=below.at[slot, at, view],
-                    send_sem=bel_s.at[delta], recv_sem=bel_r.at[slot, at],
+                    send_sem=bel_s.at[delta], recv_sem=sem,
                     device_id=(((x + delta) % chips) * 2 + k, c), device_id_type=MESH,
                 ).start()
 
@@ -143,6 +144,24 @@
             copy = below_copy(slot, at, below.at[slot, at], mate, bel_s.at[0])
             copy.wait_recv()
             copy.start()
+
+    def pass_far(e):
+        far, count = src_of(n - 1), (cut, half - cut)[e]
+        slot, at = slot_of(chunks - 1), far % per_slab
+
+        @pl.when(passing & (far // per_slab == c % slabs))
+        def _():
+            both_ways = below.at[slot, at, pl.ds(0, 2 * count)]
+            pltpu.make_async_remote_copy(
+                src_ref=both_ways, dst_ref=both_ways, send_sem=bel_s.at[0], recv_sem=bel_e.at[e],
+                device_id=(mate, c), device_id_type=MESH,
+            ).wait_recv()
+            for way in range(2):
+                view = below.at[slot, at, pl.ds(end_at(way, e), count)]
+                pltpu.make_async_remote_copy(
+                    src_ref=view, dst_ref=view, send_sem=bel_s.at[0], recv_sem=bel_r.at[slot, at],
+                    device_id=(mate, c), device_id_type=MESH,
+                ).start()
 
     def tile(m):
         return pl.ds(pl.multiple_of(m * tall, tall), tall)
@@ -262,7 +281,7 @@
                     below_arrived(last, at)
                     correct(last, at, lambda rows_at: outs[last, rows_at, :])
 
-        pass_below(steps - 1)
+        pass_far(1)
 
         @pl.when((x != source_x) & own_far)
         def _():
@@ -480,7 +499,14 @@
             def _():
                 for way in range(2):
                     ring_end(g, way, e, far).wait_recv()
-                    lend_part(g, far, end_at(way, e), (cut, half - cut)[e])
+
+                    @pl.when(g < chunks - 1)
+                    def _():
+                        lend_part(g, far, end_at(way, e), (cut, half - cut)[e])
+
+                    @pl.when(g == chunks - 1)
+                    def _():
+                        lend_part(g, far, end_at(way, e), (cut, half - cut)[e], bel_e.at[e])
 
         @pl.when(j == 0)
         def _():
@@ -495,7 +521,7 @@
         def _():
             lend(g, j + 1)
 
-        @pl.when((i == steps - 1) & home)
+        @pl.when((i == steps - 2) & home)
         def _():
             for s in range(last):
                 spread(s, 0)
@@ -520,20 +546,21 @@
         def _():
             a_copy(i + DEEP - 1).start()
 
-        @pl.loop(0, TILES)
-        def _(m):
-            term = jnp.dot(abuf[i % DEEP, tile(m), :], panel[g, src], preferred_element_type=jnp.float32)
-
-            @pl.when(j == 0)
-            def _():
-                acc[g % 2, tile(m), :] = term
-
-            @pl.when(j > 0)
-            def _():
-                acc[g % 2, tile(m), :] += term
-
-            @pl.when(j == n - 1)
-            def _():
+        @pl.when(j == 0)
+        def _():
+            acc[g % 2] = jnp.dot(abuf[i % DEEP], panel[g, src], preferred_element_type=jnp.float32)
+
+        @pl.when((j > 0) & (j < n - 1))
+        def _():
+            acc[g % 2] += jnp.dot(abuf[i % DEEP], panel[g, src], preferred_element_type=jnp.float32)
+
+        @pl.when(j == n - 1)
+        def _():
+            @pl.loop(0, TILES)
+            def _(m):
+                acc[g % 2, tile(m), :] += jnp.dot(
+                    abuf[i % DEEP, tile(m), :], panel[g, src], preferred_element_type=jnp.float32
+                )
                 give(g, m)
 
         @pl.when((j >= BEGIN) & (j < BEGIN + TILES) & (g > 0) & (g <= chunks - supers))
@@ -563,6 +590,7 @@
             early_send(s)
 
     gsum[...] = jnp.zeros_like(gsum)
+    pass_far(0)
     finish_last()
     fill(last, 0)
     spread(last, 0)
@@ -647,6 +675,7 @@
             dma((max(supers - 1, 1), chips)),
             dma((chips,)),
             dma((chunks, per_slab)),
+            dma((2,)),
             dma((chunks,)),
             dma((supers,)),
             dma((supers,)),

time: 145 us -> 145 us (level)
  no operation moved by 1% of the time
where the time goes in v6:
time: 145 us; the launch traced here: 144 us
  Pallas kernels  144 us (99%)
    pallas_call x1, Pallas kernels, body(): pl.pallas_call(functools.partial(kernel, (chips, n, depth), strips), out_...  142 us

profile of v6, /device:TPU:1, one launch (start us, length us, event | category | flops | bytes accessed | tf_op | source)
XLA Modules:
  0.0 144.4 jit_solution(3370132064725979133)
XLA Ops:
  0.6 142.4 %shard_map.68 = (bf16[2,3072,128]{2,1,0:T(8,128)(2,1)S(1)}, f32[2,512,128]{2,1,0:T(8,128)S(1)}) custom-call(s32[2,48]{1,0:T(2,128)} %order_hbm.1, bf16[2,768,512]{2,1,0:T(8,128)(2,1)} %factor_hbm.1, bf16[2,512,512]{2,1,0:T(8,128)(2,1)} %inverse_hbm.1, f32[2,512,128]{2,1,0:T(8,128)} %diag_hbm.1, bf16[3072,6144]{1,0:T(8,128)(2,1)} %a_ref.1), custom_call_target="tpu_custom_call" | custom-call | flops 38654705664 | bytes 150994944 | tf_op jit(solution)/shard_map/pallas_call | solution.py:638
  143.0 1.3 shard_map.69
